TPU v7x, 32 devices: a whole 2x2x4 slice. The times are simulated.
32 devices in a mesh: dp: 8 (over y, x, core), tensor: 4 (over z).
Axes of the slice: x: 2, y: 2, z: 4, core: 2. Of those that a mesh axis runs over, the one named last changes fastest.
Arguments:
- images: bfloat16 [8, 577, 1024], P('dp'), may hold values from -6 to 6
- valid_flags: int32 [8], P('dp'), may hold values from 0 to 1, as said below
- cotangent: bfloat16 [8, 577, 1024], P('dp'), may hold values from -6 to 6
- first_gain: float32 [1024], P('dp'), may hold values from 0.5 to 1.5
- first_shift: float32 [1024], P('dp'), may hold values from -1.75 to 1.75
- triple_weight: float32 [3, 1024, 1024], P(None, 'dp', 'tensor'), may hold values from -0.1875 to 0.1875
- pair_bias: float32 [2, 16, 64], P(None, 'tensor', 'dp'), may hold values from -1.75 to 1.75
- output_weight: float32 [1024, 1024], P('tensor', 'dp'), may hold values from -1.5 to 1.5
- output_bias: float32 [1024], P('dp'), may hold values from -1.75 to 1.75
- second_gain: float32 [1024], P('dp'), may hold values from 0.5 to 1.5
- second_shift: float32 [1024], P('dp'), may hold values from -1.75 to 1.75
- expand_weight: float32 [1024, 4096], P('dp', 'tensor'), may hold values from -1 to 1, as said below
- expand_bias: float32 [64, 64], P('tensor', 'dp'), may hold values from -1.75 to 1.75
- reduce_weight: float32 [4096, 1024], P('tensor', 'dp'), may hold values from -1 to 1, as said below
- reduce_bias: float32 [1024], P('dp'), may hold values from -1.75 to 1.75
- first_gain_mean: float32 [1024], P('dp'), may hold values from -6 to 6
- first_shift_mean: float32 [1024], P('dp'), may hold values from -6 to 6
- triple_weight_mean: float32 [3, 1024, 1024], P(None, 'dp', 'tensor'), may hold values from -6 to 6
- pair_bias_mean: float32 [2, 16, 64], P(None, 'tensor', 'dp'), may hold values from -6 to 6
- output_weight_mean: float32 [1024, 1024], P('tensor', 'dp'), may hold values from -6 to 6
- output_bias_mean: float32 [1024], P('dp'), may hold values from -6 to 6
- second_gain_mean: float32 [1024], P('dp'), may hold values from -6 to 6
- second_shift_mean: float32 [1024], P('dp'), may hold values from -6 to 6
- expand_weight_mean: float32 [1024, 4096], P('dp', 'tensor'), may hold values from -6 to 6
- expand_bias_mean: float32 [64, 64], P('tensor', 'dp'), may hold values from -6 to 6
- reduce_weight_mean: float32 [4096, 1024], P('tensor', 'dp'), may hold values from -6 to 6
- reduce_bias_mean: float32 [1024], P('dp'), may hold values from -6 to 6
- first_gain_square: float32 [1024], P('dp'), may hold values from 1 to 4
- first_shift_square: float32 [1024], P('dp'), may hold values from 1 to 4
- triple_weight_square: float32 [3, 1024, 1024], P(None, 'dp', 'tensor'), may hold values from 1 to 4
- pair_bias_square: float32 [2, 16, 64], P(None, 'tensor', 'dp'), may hold values from 1 to 4
- output_weight_square: float32 [1024, 1024], P('tensor', 'dp'), may hold values from 1 to 4
- output_bias_square: float32 [1024], P('dp'), may hold values from 1 to 4
- second_gain_square: float32 [1024], P('dp'), may hold values from 1 to 4
- second_shift_square: float32 [1024], P('dp'), may hold values from 1 to 4
- expand_weight_square: float32 [1024, 4096], P('dp', 'tensor'), may hold values from 1 to 4
- expand_bias_square: float32 [64, 64], P('tensor', 'dp'), may hold values from 1 to 4
- reduce_weight_square: float32 [4096, 1024], P('tensor', 'dp'), may hold values from 1 to 4
- reduce_bias_square: float32 [1024], P('dp'), may hold values from 1 to 4
Outputs:
- block_output: bfloat16 [8, 577, 1024], P('dp')
- input_grad: float32 [8, 577, 1024], P('dp')
- grad_norm: float32 [], replicated
- new_first_gain: float32 [1024], P('dp')
- mean_first_gain: float32 [1024], P('dp')
- square_first_gain: float32 [1024], P('dp')
- copy_first_gain: bfloat16 [1024], P('dp')
- new_first_shift: float32 [1024], P('dp')
- mean_first_shift: float32 [1024], P('dp')
- square_first_shift: float32 [1024], P('dp')
- copy_first_shift: bfloat16 [1024], P('dp')
- new_triple_weight: float32 [3, 1024, 1024], P(None, 'dp', 'tensor')
- mean_triple_weight: float32 [3, 1024, 1024], P(None, 'dp', 'tensor')
- square_triple_weight: float32 [3, 1024, 1024], P(None, 'dp', 'tensor')
- copy_triple_weight: bfloat16 [3, 1024, 1024], P(None, 'dp', 'tensor')
- new_pair_bias: float32 [2, 16, 64], P(None, 'tensor', 'dp')
- mean_pair_bias: float32 [2, 16, 64], P(None, 'tensor', 'dp')
- square_pair_bias: float32 [2, 16, 64], P(None, 'tensor', 'dp')
- copy_pair_bias: bfloat16 [2, 16, 64], P(None, 'tensor', 'dp')
- new_output_weight: float32 [1024, 1024], P('tensor', 'dp')
- mean_output_weight: float32 [1024, 1024], P('tensor', 'dp')
- square_output_weight: float32 [1024, 1024], P('tensor', 'dp')
- copy_output_weight: bfloat16 [1024, 1024], P('tensor', 'dp')
- new_output_bias: float32 [1024], P('dp')
- mean_output_bias: float32 [1024], P('dp')
- square_output_bias: float32 [1024], P('dp')
- copy_output_bias: bfloat16 [1024], P('dp')
- new_second_gain: float32 [1024], P('dp')
- mean_second_gain: float32 [1024], P('dp')
- square_second_gain: float32 [1024], P('dp')
- copy_second_gain: bfloat16 [1024], P('dp')
- new_second_shift: float32 [1024], P('dp')
- mean_second_shift: float32 [1024], P('dp')
- square_second_shift: float32 [1024], P('dp')
- copy_second_shift: bfloat16 [1024], P('dp')
- new_expand_weight: float32 [1024, 4096], P('dp', 'tensor')
- mean_expand_weight: float32 [1024, 4096], P('dp', 'tensor')
- square_expand_weight: float32 [1024, 4096], P('dp', 'tensor')
- copy_expand_weight: bfloat16 [1024, 4096], P('dp', 'tensor')
- new_expand_bias: float32 [64, 64], P('tensor', 'dp')
- mean_expand_bias: float32 [64, 64], P('tensor', 'dp')
- square_expand_bias: float32 [64, 64], P('tensor', 'dp')
- copy_expand_bias: bfloat16 [64, 64], P('tensor', 'dp')
- new_reduce_weight: float32 [4096, 1024], P('tensor', 'dp')
- mean_reduce_weight: float32 [4096, 1024], P('tensor', 'dp')
- square_reduce_weight: float32 [4096, 1024], P('tensor', 'dp')
- copy_reduce_weight: bfloat16 [4096, 1024], P('tensor', 'dp')
- new_reduce_bias: float32 [1024], P('dp')
- mean_reduce_bias: float32 [1024], P('dp')
- square_reduce_bias: float32 [1024], P('dp')
- copy_reduce_bias: bfloat16 [1024], P('dp')
Inputs may be any that keep to these rules, and one draw needn't show every extreme that they name: `valid_flags`: at least one image is blank; blank images may stand anywhere in the batch. `expand_weight`: a projection matrix with entries of order one over the root of 1024. `reduce_weight`: a projection matrix with entries of order one over the root of 4096.
All inputs are finite; a program needn't handle non-finite values.
Results may differ from a plain program's by a relative error of at most 0.012.
The roundings to bfloat16 on the way count: a program that leaves them out, or rounds other values in their place, can miss the bound.
Values may be sent and summed in bfloat16 or wider, within the bound.
A program may use at most 128 MiB of HBM per device.

v0:
```python
import math

import jax
import jax.numpy as jnp
from jax import lax
from jax.sharding import PartitionSpec as P

D = 1024
FF = 4096


shard_dims = (0, 0, 1, 2, 1, 0, 0, 0, 0, 1, 1, 0)
shared_terms = (1, 1, 0, 0, 0, 1, 1, 1, 0, 0, 0, 1)
rates = (0.2, 0.2, 0.03, 0.2, 0.03, 0.2, 0.2, 0.2, 0.03, 0.2, 0.03, 0.2)


def apply_layer_norm(input_row_block, norm_gain, norm_bias):
    center = jnp.mean(input_row_block, axis=-1, keepdims=True)
    centered_rows = input_row_block - center
    inverse_deviation = lax.rsqrt(
        jnp.mean(centered_rows * centered_rows, axis=-1, keepdims=True) + 1e-06
    )
    standardized_rows = centered_rows * inverse_deviation
    return (
        standardized_rows * norm_gain.astype(jnp.float32) + norm_bias.astype(jnp.float32),
        standardized_rows,
        inverse_deviation,
    )


def layer_norm_backward(incoming_gradient, standardized_rows, inverse_deviation, norm_gain):
    scaled_rows = incoming_gradient * norm_gain.astype(jnp.float32)
    return inverse_deviation * (
        scaled_rows
        - jnp.mean(scaled_rows, axis=-1, keepdims=True)
        - standardized_rows * jnp.mean(scaled_rows * standardized_rows, axis=-1, keepdims=True)
    )


def contract_rows(left, right):
    return lax.dot_general(
        left, right, (((0,), (0,)), ((), ())), preferred_element_type=jnp.float32
    )


def against(left, right):
    return lax.dot_general(
        left, right, (((1,), (1,)), ((), ())), preferred_element_type=jnp.float32
    )


def exact_gelu(values):
    return jax.nn.gelu(values, approximate=False)


def image_forward(parts):
    query, keys, values = parts
    factor = float(query.shape[2]) ** (-0.5)
    scores = jnp.einsum("qhd,khd->hqk", query, keys, preferred_element_type=jnp.float32) * factor
    top = jnp.max(scores, axis=-1, keepdims=True)
    totals = jnp.sum(jnp.exp(scores - top), axis=-1, keepdims=True)
    logsum = top + jnp.log(totals)
    probs = jnp.exp(scores - logsum).astype(jnp.bfloat16)
    mixed = jnp.einsum("hqk,khd->qhd", probs, values, preferred_element_type=jnp.float32)
    return (mixed.astype(jnp.bfloat16), logsum)


def image_backward(parts):
    query, keys, values, logsum, grad_mixed = parts
    factor = float(query.shape[2]) ** (-0.5)
    scores = jnp.einsum("qhd,khd->hqk", query, keys, preferred_element_type=jnp.float32) * factor
    probs = jnp.exp(scores - logsum)
    grad_probs = jnp.einsum("qhd,khd->hqk", grad_mixed, values, preferred_element_type=jnp.float32)
    grad_scores = probs * (grad_probs - jnp.sum(probs * grad_probs, axis=-1, keepdims=True))
    rounded = grad_scores.astype(jnp.bfloat16)
    grad_query = (
        jnp.einsum("hqk,khd->qhd", rounded, keys, preferred_element_type=jnp.float32) * factor
    )
    grad_keys = (
        jnp.einsum("hqk,qhd->khd", rounded, query, preferred_element_type=jnp.float32) * factor
    )
    grad_values = jnp.einsum(
        "hqk,qhd->khd", probs.astype(jnp.bfloat16), grad_mixed, preferred_element_type=jnp.float32
    )
    return (
        grad_query.astype(jnp.bfloat16),
        grad_keys.astype(jnp.bfloat16),
        grad_values.astype(jnp.bfloat16),
    )


def squared_total(grads, tensor_count):
    total = jnp.zeros((), jnp.float32)
    for incoming_gradient, shared in zip(grads, shared_terms):
        weight = 1.0 / tensor_count if shared else 1.0
        total = total + weight * jnp.sum(incoming_gradient * incoming_gradient)
    return total


def adam_step(master, row_mean, square, incoming_gradient, rate):
    mean_new = 0.5 * row_mean + 0.5 * incoming_gradient
    square_new = 0.5 * square + 0.5 * incoming_gradient * incoming_gradient
    change = -rate * (mean_new / (jnp.sqrt(square_new) + 1e-08) + 0.1 * master)
    updated = master + change
    return [updated, mean_new, square_new, updated.astype(jnp.bfloat16)]


def per_device(
    images,
    valid_flags,
    cotangent,
    first_gain,
    first_shift,
    triple_weight,
    pair_bias,
    output_weight,
    output_bias,
    second_gain,
    second_shift,
    expand_weight,
    expand_bias,
    reduce_weight,
    reduce_bias,
    first_gain_mean,
    first_shift_mean,
    triple_weight_mean,
    pair_bias_mean,
    output_weight_mean,
    output_bias_mean,
    second_gain_mean,
    second_shift_mean,
    expand_weight_mean,
    expand_bias_mean,
    reduce_weight_mean,
    reduce_bias_mean,
    first_gain_square,
    first_shift_square,
    triple_weight_square,
    pair_bias_square,
    output_weight_square,
    output_bias_square,
    second_gain_square,
    second_shift_square,
    expand_weight_square,
    expand_bias_square,
    reduce_weight_square,
    reduce_bias_square,
):
    masters = (
        first_gain,
        first_shift,
        triple_weight,
        pair_bias,
        output_weight,
        output_bias,
        second_gain,
        second_shift,
        expand_weight,
        expand_bias,
        reduce_weight,
        reduce_bias,
    )
    means = (
        first_gain_mean,
        first_shift_mean,
        triple_weight_mean,
        pair_bias_mean,
        output_weight_mean,
        output_bias_mean,
        second_gain_mean,
        second_shift_mean,
        expand_weight_mean,
        expand_bias_mean,
        reduce_weight_mean,
        reduce_bias_mean,
    )
    squares = (
        first_gain_square,
        first_shift_square,
        triple_weight_square,
        pair_bias_square,
        output_weight_square,
        output_bias_square,
        second_gain_square,
        second_shift_square,
        expand_weight_square,
        expand_bias_square,
        reduce_weight_square,
        reduce_bias_square,
    )
    rounded = tuple((master.astype(jnp.bfloat16) for master in masters))
    (
        first_norm_gain,
        first_norm_bias,
        triple,
        pairs,
        out_weight,
        out_bias,
        second_norm_gain,
        second_norm_bias,
        up_weight,
        up_bias,
        down_weight,
        down_bias,
    ) = (
        lax.all_gather(rounded[0], "dp", axis=0, tiled=True),
        lax.all_gather(rounded[1], "dp", axis=0, tiled=True),
        lax.all_gather(rounded[2], "dp", axis=1, tiled=True),
        lax.all_gather(rounded[3], "dp", axis=2, tiled=True),
        lax.all_gather(rounded[4], "dp", axis=1, tiled=True),
        lax.all_gather(rounded[5], "dp", axis=0, tiled=True),
        lax.all_gather(rounded[6], "dp", axis=0, tiled=True),
        lax.all_gather(rounded[7], "dp", axis=0, tiled=True),
        lax.all_gather(rounded[8], "dp", axis=0, tiled=True),
        lax.all_gather(rounded[9], "dp", axis=1, tiled=True),
        lax.all_gather(rounded[10], "dp", axis=1, tiled=True),
        lax.all_gather(rounded[11], "dp", axis=0, tiled=True),
    )
    shape = images.shape
    count = shape[0] * shape[1]
    heads_local = pairs.shape[1]
    head_size = pairs.shape[2]
    split = (shape[0], shape[1], heads_local, head_size)
    tensor_count = lax.axis_size("tensor")
    input_row_block = images.reshape(count, shape[2]).astype(jnp.float32)
    first_normed_rows, first_standardized, first_inverse_deviation = apply_layer_norm(
        input_row_block, first_norm_gain, first_norm_bias
    )
    inputs_one = first_normed_rows.astype(jnp.bfloat16)
    projected = jnp.einsum("td,cde->cte", inputs_one, triple, preferred_element_type=jnp.float32)
    pair_flat = pairs.reshape(2, -1).astype(jnp.float32)
    query = (projected[0] + pair_flat[0]).astype(jnp.bfloat16).reshape(split)
    keys = projected[1].astype(jnp.bfloat16).reshape(split)
    values = (projected[2] + pair_flat[1]).astype(jnp.bfloat16).reshape(split)
    mixed, logsum = lax.map(image_forward, (query, keys, values))
    mixed_flat = mixed.reshape(count, -1)
    attn_part = jnp.dot(mixed_flat, out_weight, preferred_element_type=jnp.float32)
    middle_state = input_row_block + lax.psum(attn_part, "tensor") + out_bias.astype(jnp.float32)
    second_normed_rows, second_standardized, second_inverse_deviation = apply_layer_norm(
        middle_state, second_norm_gain, second_norm_bias
    )
    inputs_two = second_normed_rows.astype(jnp.bfloat16)
    hidden = jnp.dot(inputs_two, up_weight, preferred_element_type=jnp.float32) + up_bias.reshape(
        -1
    ).astype(jnp.float32)
    active_full, gelu_back = jax.vjp(exact_gelu, hidden)
    active = active_full.astype(jnp.bfloat16)
    mlp_part = jnp.dot(active, down_weight, preferred_element_type=jnp.float32)
    result = middle_state + lax.psum(mlp_part, "tensor") + down_bias.astype(jnp.float32)
    block_output = result.astype(jnp.bfloat16)
    output_gradient = (
        cotangent.astype(jnp.float32) * valid_flags.astype(jnp.float32)[:, None, None]
    ).reshape(count, -1)
    grad_low = output_gradient.astype(jnp.bfloat16)
    grad_down_bias = jnp.sum(output_gradient, axis=0)
    grad_down_weight = contract_rows(active, grad_low)
    grad_active = against(grad_low, down_weight)
    grad_hidden = gelu_back(grad_active)[0]
    grad_up_bias = jnp.sum(grad_hidden, axis=0).reshape(up_bias.shape)
    hidden_low = grad_hidden.astype(jnp.bfloat16)
    grad_up_weight = contract_rows(inputs_two, hidden_low)
    second_normed_gradient = lax.psum(against(hidden_low, up_weight), "tensor")
    second_gain_gradient = jnp.sum(second_normed_gradient * second_standardized, axis=0)
    grad_shift_two = jnp.sum(second_normed_gradient, axis=0)
    middle_gradient = output_gradient + layer_norm_backward(
        second_normed_gradient, second_standardized, second_inverse_deviation, second_norm_gain
    )
    grad_out_bias = jnp.sum(middle_gradient, axis=0)
    middle_low = middle_gradient.astype(jnp.bfloat16)
    grad_out_weight = contract_rows(mixed_flat, middle_low)
    grad_mixed = against(middle_low, out_weight).astype(jnp.bfloat16).reshape(split)
    grad_query, grad_keys, grad_values = lax.map(
        image_backward, (query, keys, values, logsum, grad_mixed)
    )
    stacked = jnp.stack(
        [
            grad_query.reshape(count, -1),
            grad_keys.reshape(count, -1),
            grad_values.reshape(count, -1),
        ]
    )
    grad_pairs = jnp.stack(
        [
            jnp.sum(stacked[0].astype(jnp.float32), axis=0),
            jnp.sum(stacked[2].astype(jnp.float32), axis=0),
        ]
    ).reshape(pairs.shape)
    grad_triple = jnp.einsum("td,cte->cde", inputs_one, stacked, preferred_element_type=jnp.float32)
    back_one = jnp.einsum("cte,cde->td", stacked, triple, preferred_element_type=jnp.float32)
    first_normed_gradient = lax.psum(back_one, "tensor")
    first_gain_gradient = jnp.sum(first_normed_gradient * first_standardized, axis=0)
    grad_shift_one = jnp.sum(first_normed_gradient, axis=0)
    row_gradient = middle_gradient + layer_norm_backward(
        first_normed_gradient, first_standardized, first_inverse_deviation, first_norm_gain
    )
    grads = (
        first_gain_gradient,
        grad_shift_one,
        grad_triple,
        grad_pairs,
        grad_out_weight,
        grad_out_bias,
        second_gain_gradient,
        grad_shift_two,
        grad_up_weight,
        grad_up_bias,
        grad_down_weight,
        grad_down_bias,
    )
    summed = lax.psum(
        (
            grads[0],
            grads[1],
            grads[2],
            grads[3],
            grads[4],
            grads[5],
            grads[6],
            grads[7],
            grads[8],
            grads[9],
            grads[10],
            grads[11],
        ),
        "dp",
    )
    total = lax.psum(squared_total(summed, tensor_count), "tensor")
    position = lax.axis_index("dp")
    owned = tuple(
        (
            lax.dynamic_slice_in_dim(
                incoming_gradient, position * master.shape[dim], master.shape[dim], dim
            )
            for incoming_gradient, master, dim in zip(summed, masters, shard_dims)
        )
    )
    norm_value = jnp.sqrt(total)
    limit = math.sqrt(4 * D * D + 2 * D * FF + 8 * D + FF)
    factor = jnp.minimum(1.0, limit / (norm_value + 1e-06))
    updates = []
    for master, row_mean, square, incoming_gradient, rate in zip(
        masters, means, squares, owned, rates
    ):
        updates.extend(adam_step(master, row_mean, square, incoming_gradient * factor, rate))
    return (block_output.reshape(shape), row_gradient.reshape(shape), norm_value, *updates)


def solution(mesh):
    in_specs = (
        P("dp", None, None),
        P("dp"),
        P("dp", None, None),
        P("dp"),
        P("dp"),
        P(None, "dp", "tensor"),
        P(None, "tensor", "dp"),
        P("tensor", "dp"),
        P("dp"),
        P("dp"),
        P("dp"),
        P("dp", "tensor"),
        P("tensor", "dp"),
        P("tensor", "dp"),
        P("dp"),
        P("dp"),
        P("dp"),
        P(None, "dp", "tensor"),
        P(None, "tensor", "dp"),
        P("tensor", "dp"),
        P("dp"),
        P("dp"),
        P("dp"),
        P("dp", "tensor"),
        P("tensor", "dp"),
        P("tensor", "dp"),
        P("dp"),
        P("dp"),
        P("dp"),
        P(None, "dp", "tensor"),
        P(None, "tensor", "dp"),
        P("tensor", "dp"),
        P("dp"),
        P("dp"),
        P("dp"),
        P("dp", "tensor"),
        P("tensor", "dp"),
        P("tensor", "dp"),
        P("dp"),
    )
    out_specs = (
        P("dp", None, None),
        P("dp", None, None),
        P(),
        P("dp"),
        P("dp"),
        P("dp"),
        P("dp"),
        P("dp"),
        P("dp"),
        P("dp"),
        P("dp"),
        P(None, "dp", "tensor"),
        P(None, "dp", "tensor"),
        P(None, "dp", "tensor"),
        P(None, "dp", "tensor"),
        P(None, "tensor", "dp"),
        P(None, "tensor", "dp"),
        P(None, "tensor", "dp"),
        P(None, "tensor", "dp"),
        P("tensor", "dp"),
        P("tensor", "dp"),
        P("tensor", "dp"),
        P("tensor", "dp"),
        P("dp"),
        P("dp"),
        P("dp"),
        P("dp"),
        P("dp"),
        P("dp"),
        P("dp"),
        P("dp"),
        P("dp"),
        P("dp"),
        P("dp"),
        P("dp"),
        P("dp", "tensor"),
        P("dp", "tensor"),
        P("dp", "tensor"),
        P("dp", "tensor"),
        P("tensor", "dp"),
        P("tensor", "dp"),
        P("tensor", "dp"),
        P("tensor", "dp"),
        P("tensor", "dp"),
        P("tensor", "dp"),
        P("tensor", "dp"),
        P("tensor", "dp"),
        P("dp"),
        P("dp"),
        P("dp"),
        P("dp"),
    )
    return jax.shard_map(
        per_device, mesh=mesh, in_specs=in_specs, out_specs=out_specs, check_vma=False
    )
```

profile of v0, /device:TPU:0, one launch (start us, length us, event | category | flops | bytes accessed | tf_op | source)
XLA Modules:
  0.0 777.9 jit_solution(4180550084816320558)
XLA Ops:
  9.8 10.3 %all-gather.1 = bf16[8,1,128]{2,1,0:T(2,128)(2,1)S(1)} all-gather(bf16[1,1,128]{2,1,0:T(2,128)(2,1)S(1)} %convert_bitcast_fusion.5), channel_id=1, replica_groups=mesh['dp'=8,'tensor'=4] {'dp'}, dimensions={0}, use_global_device_ids=true | all-gather | bytes 2304 | tf_op jit(solution)/shard_map/all_gather | solution.py:207
  20.7 8.8 %all-gather = bf16[8,1,128]{2,1,0:T(2,128)(2,1)S(1)} all-gather(bf16[1,1,128]{2,1,0:T(2,128)(2,1)S(1)} %convert_bitcast_fusion.6), channel_id=1, replica_groups=mesh['dp'=8,'tensor'=4] {'dp'}, dimensions={0}, use_global_device_ids=true | all-gather | bytes 2304 | tf_op jit(solution)/shard_map/all_gather | solution.py:206
  30.3 8.1 %all_gather.39 = bf16[2,4,64]{1,0,2:T(2,128)(2,1)S(1)} all-gather(bf16[2,4,8]{1,0,2:T(2,128)(2,1)S(1)} %copy.199), channel_id=1, replica_groups=mesh['dp'=8,'tensor'=4] {'dp'}, dimensions={2}, use_global_device_ids=true | all-gather | bytes 1152 | tf_op jit(solution)/shard_map/all_gather | solution.py:209
  39.5 10.1 %all_gather.40 = bf16[256,1024]{1,0:T(8,128)(2,1)S(1)} all-gather(bf16[256,128]{1,0:T(8,128)(2,1)S(1)} %convert_element_type.217), channel_id=1, replica_groups=mesh['dp'=8,'tensor'=4] {'dp'}, dimensions={1}, use_global_device_ids=true | all-gather | bytes 589824 | tf_op jit(solution)/shard_map/all_gather | solution.py:210
  65.6 7.8 %all-gather.2 = bf16[8,1,128]{2,1,0:T(2,128)(2,1)S(1)} all-gather(bf16[1,1,128]{2,1,0:T(2,128)(2,1)S(1)} %convert_bitcast_fusion.4), channel_id=1, replica_groups=mesh['dp'=8,'tensor'=4] {'dp'}, dimensions={0}, use_global_device_ids=true | all-gather | bytes 2304 | tf_op jit(solution)/shard_map/all_gather | solution.py:211
  73.5 8.9 %all_gather.45 = bf16[16,64]{0,1:T(8,128)(2,1)S(1)} all-gather(bf16[16,8]{0,1:T(8,128)(2,1)S(1)} %convert_element_type.226), channel_id=1, replica_groups=mesh['dp'=8,'tensor'=4] {'dp'}, dimensions={1}, use_global_device_ids=true | all-gather | bytes 2304 | tf_op jit(solution)/shard_map/all_gather | solution.py:215
  82.5 7.8 %all-gather.4 = bf16[8,1,128]{2,1,0:T(2,128)(2,1)S(1)} all-gather(bf16[1,1,128]{2,1,0:T(2,128)(2,1)S(1)} %convert_bitcast_fusion.2), channel_id=1, replica_groups=mesh['dp'=8,'tensor'=4] {'dp'}, dimensions={0}, use_global_device_ids=true | all-gather | bytes 2304 | tf_op jit(solution)/shard_map/all_gather | solution.py:213
  90.3 8.9 %all-gather.3 = bf16[8,1,128]{2,1,0:T(2,128)(2,1)S(1)} all-gather(bf16[1,1,128]{2,1,0:T(2,128)(2,1)S(1)} %convert_bitcast_fusion.3), channel_id=1, replica_groups=mesh['dp'=8,'tensor'=4] {'dp'}, dimensions={0}, use_global_device_ids=true | all-gather | bytes 2304 | tf_op jit(solution)/shard_map/all_gather | solution.py:212
  99.9 60.0 %all-reduce.8.cloned.1.call-done = f32[577,1024]{1,0:T(8,128)} async-done(((f32[577,1024]{1,0:T(8,128)}), f32[577,1024]{1,0:T(8,128)}) %all-reduce.8.cloned.1.call-update) | async-done | bytes 2363408 | tf_op jit(solution)/shard_map/psum | solution.py:238
  162.8 26.4 %all-gather.12.cloned.1.call-done = bf16[1024,1024]{1,0:T(8,128)(2,1)} async-done(((bf16[128,1024]{1,0:T(8,128)(2,1)}), bf16[1024,1024]{1,0:T(8,128)(2,1)}) %all-gather.12.cloned.1.call-update) | async-done | bytes 2097168 | tf_op jit(solution)/shard_map/all_gather | solution.py:214
  189.2 10.2 %multiply_convert_fusion.1 = (bf16[577,1024]{1,0:T(8,128)(2,1)}, f32[577,1024]{1,0:T(8,128)}, f32[577,1024]{1,0:T(8,128)}) fusion(f32[1024]{0:T(1024)S(1)} %reshape.236, bf16[1024,1024]{1,0:T(8,128)(2,1)} %all-gather.12.cloned.1.call-done, f32[577,1024]{1,0:T(8,128)S(1)} %get-tuple-element.426, f32[1024]{0:T(1024)S(1)} %bitcast.159, ...), kind=kOutput, calls=%fused_computation.39 | convolution fusion | flops 1252006912 | bytes 10385928 | tf_op jit(solution)/shard_map/dot_general | solution.py:243
  199.4 20.3 %all-gather.14.cloned.1.call-done = bf16[1024,1024]{1,0:T(8,128)(2,1)} async-done(((bf16[1024,128]{1,0:T(8,128)(2,1)}), bf16[1024,1024]{1,0:T(8,128)(2,1)}) %all-gather.14.cloned.1.call-update) | async-done | bytes 2097168 | tf_op jit(solution)/shard_map/all_gather | solution.py:216
  219.7 5.7 fusion.92
  229.7 4.9 fusion.94
  234.5 90.8 %all-reduce.10.cloned.1.call-done = f32[577,1024]{1,0:T(8,128)} async-done(((f32[577,1024]{1,0:T(8,128)}), f32[577,1024]{1,0:T(8,128)}) %all-reduce.10.cloned.1.call-update) | async-done | bytes 2363408 | tf_op jit(solution)/shard_map/psum | solution.py:262
  333.8 4.8 convert_reduce_fusion.1
  355.1 5.7 fusion.30
  375.9 152.1 %all-reduce.14.cloned.1.call-done = (f32[577,1024]{1,0:T(8,128)}, f32[577,1024]{1,0:T(8,128)}) async-done(((f32[577,1024]{1,0:T(8,128)}, f32[577,1024]{1,0:T(8,128)}), (f32[577,1024]{1,0:T(8,128)}, f32[577,1024]{1,0:T(8,128)})) %all-reduce.14.cloned.1.call-update) | async-done | bytes 4726800 | tf_op jit(solution)/shard_map/psum | solution.py:249
  531.1 26.6 %all-reduce = (f32[1024]{0:T(1024)S(1)}, f32[1024]{0:T(1024)S(1)}, f32[2,4,64]{2,1,0:T(4,128)S(1)}, f32[1024]{0:T(1024)S(1)}, f32[1024]{0:T(1024)S(1)}, /*index=...) all-reduce(f32[1024]{0:T(1024)S(1)} %get-tuple-element.353, ...), channel_id=1, replica_groups=mesh['dp'=8,'tensor'=4] {'dp'}, use_global_device_ids=true, to_apply=%region_16.17 | all-reduce | flops 7680 | bytes 61440 | tf_op jit(solution)/shard_map/psum | solution.py:310
  566.4 5.5 fusion.15
  571.9 132.6 %all-reduce.12.cloned.1.call-done = (f32[3,1024,256]{1,2,0:T(8,128)}, f32[256,1024]{1,0:T(8,128)}, f32[1024,1024]{1,0:T(8,128)}, f32[1024,1024]{1,0:T(8,128)}) async-done(((f32[3,1024,256]{1,2,0:T(8,128)}, f32[256,1024]{1,0:T(8,128)}, f32[1024,1024]{1,0:T(8,128)}, f32[1024,1024]{1,0:T(8,128)}), (f32[3,1024,256]{1,2,0:T(8,128)}, f32[256,1024]{1,0:T(8,128)}, f32[1024,1024]{1,0:T(8,128)}, ...) | async-done | bytes 12582928 | tf_op jit(solution)/shard_map/psum | solution.py:310
  717.5 5.5 copy.218
  723.0 12.2 %psum.135 = f32[]{:T(128)} all-reduce(f32[]{:T(128)S(6)} %add.421), channel_id=1, replica_groups=mesh['dp'=8,'tensor'=4] {'tensor'}, use_global_device_ids=true, to_apply=%region_48.49 | all-reduce | flops 1 | bytes 8 | tf_op jit(solution)/shard_map/psum | solution.py:327
  736.6 8.7 %all-gather.5 = bf16[8,1,128]{2,1,0:T(2,128)(2,1)S(1)} all-gather(bf16[1,1,128]{2,1,0:T(2,128)(2,1)S(1)} %get-tuple-element.431), channel_id=1, replica_groups=mesh['dp'=8,'tensor'=4] {'dp'}, dimensions={0}, use_global_device_ids=true | all-gather | bytes 2304 | tf_op jit(solution)/shard_map/all_gather | solution.py:217
  (232 shorter events, 109.4 us)
Async XLA Ops:
  7.2 42.4 %copy-start.3 = (bf16[1,577,1024]{2,1,0:T(8,128)(2,1)S(1)}, bf16[1,577,1024]{2,1,0:T(8,128)(2,1)}, u32[]{:S(2)}) copy-start(bf16[1,577,1024]{2,1,0:T(8,128)(2,1)} %param.39) | copy-start | bytes 3545092
  7.3 43.2 %all-gather.10.cloned.1.call-start = ((), (), s32[]{:S(2)}) async-start(), calls=%async_computation | async-start | bytes 1769472 | tf_op jit(solution)/shard_map/all_gather | solution.py:208
  9.1 150.9 %all-reduce.8.cloned.1.call-start = ((), (), s32[]{:S(2)}) async-start(), calls=%async_computation.1 | async-start | bytes 4784128 | tf_op jit(solution)/shard_map/psum | solution.py:238
  49.7 12.1 %copy-start.11 = (bf16[256,1024]{1,0:T(8,128)(2,1)}, bf16[256,1024]{1,0:T(8,128)(2,1)S(1)}, u32[]{:S(2)}) copy-start(bf16[256,1024]{1,0:T(8,128)(2,1)S(1)} %all_gather.40) | copy-start | bytes 1572868
  63.8 9.7 %copy-start.31 = (f32[16,8]{0,1:T(8,128)S(1)}, f32[16,8]{0,1:T(8,128)}, u32[]{:S(2)}) copy-start(f32[16,8]{0,1:T(8,128)} %param.51) | copy-start | bytes 1540
  63.8 18.7 %copy-start.48 = (f32[128]{0:T(128)S(1)}, f32[128]{0:T(128)}, u32[]{:S(2)}) copy-start(f32[128]{0:T(128)} %param.49) | copy-start | bytes 1540
  63.8 26.6 %copy-start.45 = (f32[128]{0:T(128)S(1)}, f32[128]{0:T(128)}, u32[]{:S(2)}) copy-start(f32[128]{0:T(128)} %param.48) | copy-start | bytes 1540
  63.8 125.4 %all-gather.12.cloned.1.call-start = ((), (), s32[]{:S(2)}) async-start(), calls=%async_computation.2 | async-start | bytes 2359296 | tf_op jit(solution)/shard_map/all_gather | solution.py:214
  64.6 155.1 %all-gather.14.cloned.1.call-start = ((), (), s32[]{:S(2)}) async-start(), calls=%async_computation.3 | async-start | bytes 2359296 | tf_op jit(solution)/shard_map/all_gather | solution.py:216
  65.6 259.8 %all-reduce.10.cloned.1.call-start = ((), (), s32[]{:S(2)}) async-start(), calls=%async_computation.4 | async-start | bytes 4784128 | tf_op jit(solution)/shard_map/psum | solution.py:262
  229.4 298.6 %all-reduce.14.cloned.1.call-start = ((), (), s32[]{:S(2)}) async-start(), calls=%async_computation.6 | async-start | bytes 9568256 | tf_op jit(solution)/shard_map/psum | solution.py:249
  333.7 9.3 %slice-start = ((s8[5980160]{0:T(1024)(128)(4,1)}), s8[4194304]{0:T(1024)(128)(4,1)S(1)}, s32[]{:S(2)}) async-start(s8[5980160]{0:T(1024)(128)(4,1)} %bitcast.128), calls=%async_computation.7 | async-start | bytes 8388608
  354.8 349.7 %all-reduce.12.cloned.1.call-start = ((), (), s32[]{:S(2)}) async-start(), calls=%async_computation.5 | async-start | bytes 25165824 | tf_op jit(solution)/shard_map/psum | solution.py:310
  713.5 22.4 %copy-start.51 = (f32[128]{0:T(128)S(1)}, f32[128]{0:T(128)}, u32[]{:S(2)}) copy-start(f32[128]{0:T(128)} %param.53) | copy-start | bytes 1540
  713.5 22.4 %copy-start.52 = (f32[128]{0:T(128)S(1)}, f32[128]{0:T(128)}, u32[]{:S(2)}) copy-start(f32[128]{0:T(128)} %param.77) | copy-start | bytes 1540
  713.5 22.4 %copy-start.53 = (f32[128]{0:T(128)S(1)}, f32[128]{0:T(128)}, u32[]{:S(2)}) copy-start(f32[128]{0:T(128)} %param.65) | copy-start | bytes 1540
  754.3 8.0 %copy-start.49 = (f32[128]{0:T(128)S(1)}, f32[128]{0:T(128)}, u32[]{:S(2)}) copy-start(f32[128]{0:T(128)} %param.73) | copy-start | bytes 1540
  754.3 8.0 %copy-start.50 = (f32[128]{0:T(128)S(1)}, f32[128]{0:T(128)}, u32[]{:S(2)}) copy-start(f32[128]{0:T(128)} %param.61) | copy-start | bytes 1540
  754.3 8.6 %copy-start.17 = (f32[128,1024]{1,0:T(8,128)S(1)}, f32[128,1024]{1,0:T(8,128)}, u32[]{:S(2)}) copy-start(f32[128,1024]{1,0:T(8,128)} %param.50) | copy-start | bytes 1572868
  754.3 8.6 %copy-start.22 = (f32[128,1024]{1,0:T(8,128)S(1)}, f32[128,1024]{1,0:T(8,128)}, u32[]{:S(2)}) copy-start(f32[128,1024]{1,0:T(8,128)} %param.74) | copy-start | bytes 1572868
  754.3 8.6 %copy-start.23 = (f32[128,1024]{1,0:T(8,128)S(1)}, f32[128,1024]{1,0:T(8,128)}, u32[]{:S(2)}) copy-start(f32[128,1024]{1,0:T(8,128)} %param.62) | copy-start | bytes 1572868
  759.2 7.6 copy-start.19
  759.2 7.6 copy-start.24
  759.2 7.6 copy-start.25
  (42 other events, 165.4 us)
Sparse Core Ops, SparseCore 0:
  10.5 28.3 all-gather.9
  63.9 96.0 all-reduce.7
  162.5 26.7 all-gather.11
  191.5 28.0 all-gather.13
  229.5 95.7 all-reduce.9
  354.9 173.0 all-reduce.13
  532.6 171.8 all-reduce.11
where the time goes:
time: 785 us; the launch traced here: 778 us
  waiting for transfers between devices  482 us (61%)
  blocking collectives  118 us (15%)
  matrix products  66.1 us (8%)
  other arithmetic  57.7 us (7%)
  local copies, waits for them, and re-layouts  27 us (3%)
  between operations  25.8 us (3%)
    psum x1, waiting for transfers between devices, per_device(): lax.psum(mlp_part, 'tensor')  152 us
    psum x1, waiting for transfers between devices, per_device(): lax.psum((grads[0], grads[1], grads[2], grads[3], grads[4], grads[5], gra...  133 us
    psum x1, waiting for transfers between devices, per_device(): second_normed_gradient = lax.psum(against(hidden_low, up_weight), 'tensor')  90.8 us
    psum x1, waiting for transfers between devices, per_device(): lax.psum(attn_part, 'tensor')  60 us
    psum x1, blocking collectives, per_device(): lax.psum((grads[0], grads[1], grads[2], grads[3], grads[4], grads[5], gra...  26.6 us
    all_gather x1, waiting for transfers between devices, per_device(): lax.all_gather(rounded[8], 'dp', axis=0, tiled=True)  26.4 us
    unnamed x126, local copies, waits for them, and re-layouts  20.7 us
    all_gather x1, waiting for transfers between devices, per_device(): lax.all_gather(rounded[10], 'dp', axis=1, tiled=True)  20.3 us
  transfers between devices with their start and end apart: 7, of which 6 were waited for; matrix products, arithmetic and copies ran while one was open for 7% of the time, Pallas kernels for 0%

commit v1 on v0

--- a/solution.py
+++ b/solution.py
@@ -1,8 +1,12 @@
+import functools
 import math
+import types
 
 import jax
 import jax.numpy as jnp
 from jax import lax
+from jax.experimental import pallas as pl
+from jax.experimental.pallas import tpu as pltpu
 from jax.sharding import PartitionSpec as P
 
 D = 1024
@@ -345,6 +349,768 @@
     return (block_output.reshape(shape), row_gradient.reshape(shape), norm_value, *updates)
 
 
+HEAD = 64
+ROWS = 640
+BLOCK = 160
+SUB = 32
+LANES = 128
+BF = jnp.bfloat16
+F32 = jnp.float32
+NEG = -1e30
+MESH = pl.DeviceIdType.MESH
+
+
+def flip(index, pattern, bits):
+    out = index
+    for bit in range(bits):
+        if (pattern >> bit) & 1:
+            step = 1 << bit
+            out = out + (1 - 2 * lax.rem(lax.div(index, step), 2)) * step
+    return out
+
+
+def nt(left, right):
+    return lax.dot_general(left, right, (((1,), (1,)), ((), ())), preferred_element_type=F32)
+
+
+def nn(left, right):
+    return jnp.dot(left, right, preferred_element_type=F32)
+
+
+def tile(index, size):
+    return pl.ds(pl.multiple_of(index * size, size), size)
+
+
+def rows32(start, size):
+    return pl.ds(pl.multiple_of(start, SUB), size)
+
+
+def center_scale(v):
+    c = v - jnp.mean(v, axis=-1, keepdims=True)
+    r = lax.rsqrt(jnp.mean(c * c, axis=-1, keepdims=True) + 1e-06)
+    return c * r, r
+
+
+SCRATCH = dict(
+    xs=((ROWS, D), BF),
+    gyb=((ROWS, D), BF),
+    small_own=((8, LANES), F32),
+    vec=((8, D), F32),
+    vecb=((8, D), F32),
+    bias3=((3, 1, 256), F32),
+    ebias=((1, D), F32),
+    wqkv=((3, D, 256), BF),
+    wof=((D, D), BF),
+    wr=((D, D), BF),
+    we=((D, D), BF),
+    a1=((ROWS, D), BF),
+    a1t=((D, ROWS), BF),
+    tt=((D, ROWS), BF),
+    qkv=((3, ROWS, 256), BF),
+    kt=((256, ROWS), BF),
+    vt=((256, ROWS), BF),
+    ot=((256, ROWS), BF),
+    of=((ROWS, D), BF),
+    lse=((4, 1, ROWS), F32),
+    x1=((ROWS, D), F32),
+    a2=((ROWS, D), BF),
+    du=((ROWS, D), F32),
+    hb=((ROWS, 256), F32),
+    u=((ROWS, D), BF),
+    dhb=((ROWS, D), BF),
+    r3s=((3, BLOCK, D), BF),
+    r3r=((3, BLOCK, D), BF),
+    r2s=((3, BLOCK, D), BF),
+    r2r=((3, BLOCK, D), BF),
+    r4s=((3, BLOCK, D), BF),
+    r4r=((3, BLOCK, D), BF),
+    dxf=((ROWS, D), BF),
+    dobs=((3, BLOCK, 256), BF),
+    dob=((ROWS, 256), BF),
+    ds4=((ROWS, 512), BF),
+    p4=((ROWS, 512), BF),
+    qm4=((512, 256), BF),
+    dm4=((512, 256), BF),
+    dk=((ROWS, 256), F32),
+    dv=((ROWS, 256), F32),
+    dqt=((256, LANES), F32),
+    dqkv=((3, ROWS, 256), BF),
+    yb=((ROWS, D), BF),
+    xg=((ROWS, D), BF),
+    gwr=((D, D), BF),
+    gwe=((D, D), BF),
+    gwo=((256, D), BF),
+    gwq=((3, D, 256), BF),
+    pr_r=((4, D, LANES), BF),
+    pr_e=((4, LANES, D), BF),
+    pr_o=((4, 256, LANES), BF),
+    pr_q=((4, 3, LANES, 256), BF),
+    cr_r=((3, D, LANES), BF),
+    cr_e=((3, LANES, D), BF),
+    cr_o=((3, 256, LANES), BF),
+    cr_q=((3, 3, LANES, 256), BF),
+    sg=((8, D), F32),
+    sgz=((3, 8, D), F32),
+    sgt=((8, D), F32),
+    sgd=((7, 8, D), F32),
+    nrm=((2, 8, LANES), F32),
+    nrz=((3, 8, LANES), F32),
+    nrd=((7, 8, LANES), F32),
+)
+SEMS = dict(
+    ld=(8,),
+    g_s=(5, 8),
+    g_r=(5, 8),
+    wz_s=(3,),
+    wz_r=(3,),
+    o_s=(5, 3),
+    o_r=(5, 3),
+    z_s=(9, 3),
+    z_r=(9, 3),
+    p_s=(4, 4),
+    p_r=(4, 4),
+    c_s=(4, 3),
+    c_r=(4, 3),
+    d_s=(2, 7),
+    d_r=(2, 7),
+)
+INPUTS = dict(x_in=0, gy_in=0, small_in=0, q_in=0, o_in=0, e_in=0, r_in=0)
+OUTPUTS = dict(gq=0, go=0, ge=0, gr=0, sg_out=0, total=0, y_out=0, xg_out=0)
+
+
+def block_kernel(tokens, *refs):
+    names = (*INPUTS, *OUTPUTS, *SCRATCH, *SEMS)
+    R = types.SimpleNamespace(**dict(zip(names, refs)))
+    me = lax.axis_index("dp")
+    z = lax.axis_index("tensor")
+    dpx = [flip(me, e, 3) for e in range(8)]
+    zx = [flip(z, d, 2) for d in range(4)]
+    sent = []
+
+    def remote(src, dst, send, recv, where):
+        return pltpu.make_async_remote_copy(
+            src_ref=src, dst_ref=dst, send_sem=send, recv_sem=recv,
+            device_id=where, device_id_type=MESH,
+        )
+
+    def post(copy):
+        copy.start()
+        sent.append(copy)
+
+    barrier = pltpu.get_barrier_semaphore()
+    for e in range(1, 8):
+        pl.semaphore_signal(barrier, inc=1, device_id={"dp": dpx[e]}, device_id_type=MESH)
+    for d in range(1, 4):
+        pl.semaphore_signal(barrier, inc=1, device_id={"tensor": zx[d]}, device_id_type=MESH)
+    loads = [
+        pltpu.make_async_copy(a, b, R.ld.at[i])
+        for i, (a, b) in enumerate(
+            (
+                (R.small_in, R.small_own),
+                (R.q_in, R.gq),
+                (R.o_in, R.go),
+                (R.r_in, R.gr),
+                (R.e_in, R.ge),
+                (R.x_in, R.xs),
+                (R.gy_in, R.gyb),
+            )
+        )
+    ]
+    for copy in loads:
+        copy.start()
+
+    GATHER = {
+        "small": (0, lambda j: R.vec.at[:, tile(j, LANES)]),
+        "q": (1, lambda j: R.wqkv.at[:, tile(j, LANES), :]),
+        "o": (2, lambda j: R.wof.at[:, tile(j, LANES)]),
+        "r": (3, lambda j: R.wr.at[:, tile(j, LANES)]),
+        "e": (4, lambda j: R.we.at[tile(j, LANES), :]),
+    }
+
+    def gather_copy(name, source, target, slot):
+        a, region = GATHER[name]
+        part = region(dpx[source])
+        return remote(part, part, R.g_s.at[a, slot], R.g_r.at[a, slot], {"dp": dpx[target]})
+
+    def gather_send(name):
+        for e in (6, 2, 4, 1):
+            post(gather_copy(name, 0, e, e))
+
+    def gather_pass(name):
+        for e in (2, 4, 6):
+            gather_copy(name, e, e, e).wait_recv()
+            post(gather_copy(name, e, 1, e + 1))
+
+    def gather_wait(name):
+        for e in (1, 3, 5, 7):
+            gather_copy(name, e, 1, e).wait_recv()
+
+    own = tile(me, LANES)
+    loads[0].wait()
+    R.vec[:, own] = R.small_own[...]
+    loads[1].wait()
+    R.wqkv[:, own, :] = R.gq[...].astype(BF)
+    loads[2].wait()
+    R.wof[tile(z, 256), own] = R.go[...].astype(BF)
+    pl.semaphore_wait(barrier, 10)
+    gather_send("small")
+    gather_send("q")
+    for d in (3, 2, 1):
+        part = R.wof.at[tile(z, 256), own]
+        post(remote(part, part, R.wz_s.at[d - 1], R.wz_r.at[d - 1], {"tensor": zx[d]}))
+    loads[3].wait()
+    R.wr[:, own] = R.gr[...].astype(BF)
+    loads[4].wait()
+    R.we[own, :] = R.ge[...].astype(BF)
+    for d in (1, 2, 3):
+        part = R.wof.at[tile(zx[d], 256), own]
+        remote(part, part, R.wz_s.at[d - 1], R.wz_r.at[d - 1], {"tensor": zx[d]}).wait_recv()
+    gather_send("o")
+    gather_send("r")
+    gather_send("e")
+
+    gather_pass("small")
+    gather_wait("small")
+    R.vecb[...] = R.vec[...].astype(BF).astype(F32)
+    spread_row = lax.broadcasted_iota(jnp.int32, (LANES, D), 0)
+    spread_col = lax.broadcasted_iota(jnp.int32, (LANES, D), 1)
+    spread = jnp.where(
+        (lax.div(spread_row, 8) == lax.div(spread_col, 64))
+        & (lax.rem(spread_row, 8) == lax.rem(spread_col, 8)),
+        1.0,
+        0.0,
+    ).astype(BF)
+    turn = lax.rem(lax.div(lax.broadcasted_iota(jnp.int32, (8, D), 1), 8), 8)
+    pick = turn == lax.broadcasted_iota(jnp.int32, (8, D), 0)
+
+    def unpack(row):
+        parts = jnp.concatenate(
+            [R.vecb[row : row + 1, j * LANES : (j + 1) * LANES] for j in range(8)], axis=0
+        ).astype(BF)
+        wide = nn(parts, spread)
+        return jnp.sum(jnp.where(pick, wide, 0.0), axis=0, keepdims=True)
+
+    R.ebias[...] = unpack(6)
+    pair = unpack(7)
+    R.bias3[0] = pair[:, :256]
+    R.bias3[1] = jnp.zeros((1, 256), F32)
+    R.bias3[2] = pair[:, 256:512]
+
+    loads[5].wait()
+    gain1, shift1 = R.vecb[0:1, :], R.vecb[1:2, :]
+    sub_iota = lax.broadcasted_iota(jnp.int32, (SUB, 1), 0)
+
+    @pl.loop(0, ROWS // SUB)
+    def _(b):
+        rows = tile(b, SUB)
+        hat, _ = center_scale(R.xs[rows, :].astype(F32))
+        out = jnp.where(sub_iota + b * SUB < tokens, hat * gain1 + shift1, 0.0)
+        R.a1[rows, :] = out.astype(BF)
+
+    def flip_into(target, source):
+        @pl.loop(0, D // LANES)
+        def _(i):
+            target[tile(i, LANES), :] = source[:, tile(i, LANES)].T
+
+    flip_into(R.a1t, R.a1)
+
+    gather_pass("q")
+    gather_wait("q")
+
+    @pl.loop(0, 3)
+    def _(c):
+        acc = nn(R.a1[...], R.wqkv[c]) + R.bias3[c]
+        R.qkv[c] = acc.astype(BF)
+
+    scale = jnp.asarray(HEAD ** (-0.5), BF)
+    R.qkv[0] = R.qkv[0] * scale
+    R.kt[...] = R.qkv[1].T
+    R.vt[...] = R.qkv[2].T
+    head_lane = lax.div(lax.broadcasted_iota(jnp.int32, (LANES, 256), 1), HEAD)
+    edge = tokens // 64 * 64
+    tail_iota = lax.broadcasted_iota(jnp.int32, (ROWS - edge, LANES), 0) + edge
+
+    def masked_scores(query):
+        s = nt(R.qkv[1], query)
+        return jnp.concatenate([s[:edge], jnp.where(tail_iota < tokens, s[edge:], NEG)], axis=0)
+
+    def only_head(value, h):
+        return jnp.where(head_lane == h, value, jnp.zeros_like(value))
+
+    def o_copy(b, d, source):
+        part = R.of.at[tile(b, LANES), tile(zx[source], 256)]
+        return remote(part, part, R.o_s.at[b, d - 1], R.o_r.at[b, d - 1], {"tensor": zx[d]})
+
+    @pl.loop(0, ROWS // LANES)
+    def _(b):
+        cols = tile(b, LANES)
+        query = R.qkv[0, cols, :]
+        for h in range(4):
+            s = masked_scores(only_head(query, h))
+            top = jnp.max(s, axis=0, keepdims=True)
+            p = jnp.exp(s - top)
+            total = jnp.sum(p, axis=0, keepdims=True)
+            R.lse[h, :, cols] = top + jnp.log(total)
+            pb = (p * (1.0 / total)).astype(BF)
+            mixed = nn(R.vt[h * HEAD : (h + 1) * HEAD, :], pb)
+            R.ot[h * HEAD : (h + 1) * HEAD, cols] = mixed.astype(BF)
+        R.of[cols, tile(z, 256)] = R.ot[:, cols].T
+        for d in (3, 2, 1):
+            o_copy(b, d, 0).start()
+
+    gather_pass("o")
+    loads[6].wait()
+    gather_pass("r")
+    gather_wait("r")
+
+    @pl.loop(0, 4)
+    def _(n):
+        R.du[:, tile(n, 256)] = nt(R.gyb[...], R.wr[tile(n, 256), :])
+
+    gather_wait("o")
+    out_bias = R.vecb[2:3, :]
+    gain2, shift2 = R.vecb[3:4, :], R.vecb[4:5, :]
+
+    @pl.loop(0, ROWS // LANES)
+    def _(b):
+        rows = tile(b, LANES)
+        for d in (1, 2, 3):
+            o_copy(b, d, d).wait_recv()
+
+        @pl.loop(0, 4)
+        def _(n):
+            cols = tile(n, 256)
+            R.x1[rows, cols] = R.xs[rows, cols].astype(F32) + nn(R.of[rows, :], R.wof[:, cols])
+
+        @pl.loop(0, LANES // SUB)
+        def _(i):
+            part = rows32(b * LANES + i * SUB, SUB)
+            v = R.x1[part, :] + out_bias
+            R.x1[part, :] = v
+            hat, _ = center_scale(v)
+            R.a2[part, :] = (hat * gain2 + shift2).astype(BF)
+
+    gather_pass("e")
+    gather_wait("e")
+
+    @pl.loop(0, 4)
+    def _(n):
+        cols = tile(n, 256)
+        R.hb[...] = nn(R.a2[...], R.we[:, cols]) + R.ebias[:, cols]
+
+        def part(i, total):
+            rows = tile(i, SUB)
+            h = R.hb[rows, :]
+            cdf = 0.5 * (1.0 + lax.erf(h * math.sqrt(0.5)))
+            slope = cdf + h * (jnp.exp(-0.5 * h * h) * (1.0 / math.sqrt(2.0 * math.pi)))
+            dh = R.du[rows, cols] * slope
+            R.u[rows, cols] = (h * cdf).astype(BF)
+            R.dhb[rows, cols] = dh.astype(BF)
+            return total + jnp.sum(dh, axis=0, keepdims=True)
+
+        R.sg[6:7, cols] = lax.fori_loop(0, ROWS // SUB, part, jnp.zeros((1, 256), F32))
+
+    def z_copy(x, d, src, dst):
+        return remote(src, dst, R.z_s.at[x, d - 1], R.z_r.at[x, d - 1], {"tensor": zx[d]})
+
+    def z_scatter(x, d, s, r):
+        return z_copy(x, d, s.at[d - 1], r.at[d - 1])
+
+    for d in (3, 2, 1, 0):
+        rows = rows32(zx[d] * BLOCK, BLOCK)
+
+        @pl.loop(0, 4)
+        def _(n):
+            cols = tile(n, 256)
+            part = nt(R.dhb[rows, :], R.we[cols, :])
+            if d:
+                R.r3s[d - 1, :, cols] = part.astype(BF)
+            else:
+                R.du[0:BLOCK, cols] = part
+
+        if d:
+            post(z_scatter(0, d, R.r3s, R.r3r))
+
+    PIECES = {
+        "r": (0, R.pr_r, R.cr_r, R.gr, lambda j: R.gwr.at[:, tile(j, LANES)]),
+        "e": (1, R.pr_e, R.cr_e, R.ge, lambda j: R.gwe.at[tile(j, LANES), :]),
+        "o": (2, R.pr_o, R.cr_o, R.go, lambda j: R.gwo.at[:, tile(j, LANES)]),
+        "q": (3, R.pr_q, R.cr_q, R.gq, lambda j: R.gwq.at[:, tile(j, LANES), :]),
+    }
+
+    def pair_copy(name, t):
+        a, pr, _, _, piece = PIECES[name]
+        return remote(
+            piece(dpx[2 * t + 1]), pr.at[t], R.p_s.at[a, t], R.p_r.at[a, t], {"dp": dpx[1]}
+        )
+
+    def cross_copy(name, t):
+        a, _, cr, _, piece = PIECES[name]
+        return remote(
+            piece(dpx[2 * t]), cr.at[t - 1], R.c_s.at[a, t - 1], R.c_r.at[a, t - 1],
+            {"dp": dpx[2 * t]},
+        )
+
+    def pair_send(name):
+        for t in (3, 1, 2, 0):
+            post(pair_copy(name, t))
+
+    def pair_sum(name):
+        _, pr, _, out, piece = PIECES[name]
+        for t in (3, 1, 2, 0):
+            pair_copy(name, t).wait_recv()
+            held = piece(dpx[2 * t])
+            both = held[...].astype(F32) + pr[t].astype(F32)
+            if t:
+                held[...] = both.astype(BF)
+                post(cross_copy(name, t))
+            else:
+                out[...] = both
+
+    def cross_sum(name):
+        _, _, cr, out, _ = PIECES[name]
+        for t in (1, 2, 3):
+            cross_copy(name, t).wait_recv()
+        both = out[...] + cr[0].astype(F32) + cr[1].astype(F32) + cr[2].astype(F32)
+        out[...] = both
+        return jnp.sum(both * both)
+
+    flip_into(R.tt, R.u)
+
+    @pl.loop(0, 4)
+    def _(n):
+        R.gwr[:, tile(n, 256)] = nn(R.tt[...], R.gyb[:, tile(n, 256)]).astype(BF)
+
+    pair_send("r")
+    flip_into(R.tt, R.a2)
+
+    @pl.loop(0, 4)
+    def _(n):
+        R.gwe[:, tile(n, 256)] = nn(R.tt[...], R.dhb[:, tile(n, 256)]).astype(BF)
+
+    pair_send("e")
+    pair_sum("r")
+
+    for d in (3, 2, 1, 0):
+        rows = rows32(zx[d] * BLOCK, BLOCK)
+
+        @pl.loop(0, 4)
+        def _(n):
+            cols = tile(n, 256)
+            part = nn(R.u[rows, :], R.wr[:, cols])
+            if d:
+                R.r2s[d - 1, :, cols] = part.astype(BF)
+            else:
+                R.du[BLOCK : 2 * BLOCK, cols] = part
+
+    pair_sum("e")
+
+    mine = z * BLOCK
+    mine_rows = rows32(mine, BLOCK)
+    for d in (1, 2, 3):
+        z_scatter(0, d, R.r3s, R.r3r).wait_recv()
+
+    def norm_part(i, sums):
+        local = tile(i, SUB)
+        rows = rows32(mine + i * SUB, SUB)
+        dxn = (
+            R.du[local, :]
+            + R.r3r[0, local, :].astype(F32)
+            + R.r3r[1, local, :].astype(F32)
+            + R.r3r[2, local, :].astype(F32)
+        )
+        hat, r = center_scale(R.x1[rows, :])
+        gy = R.gyb[rows, :].astype(F32)
+        e = dxn * gain2
+        dx = gy + r * (
+            e
+            - jnp.mean(e, axis=-1, keepdims=True)
+            - hat * jnp.mean(e * hat, axis=-1, keepdims=True)
+        )
+        R.du[rows32(3 * BLOCK + i * SUB, SUB), :] = dx
+        R.dxf[rows, :] = dx.astype(BF)
+        terms = (dxn * hat, dxn, dx, gy)
+        return tuple(s + jnp.sum(t, axis=0, keepdims=True) for s, t in zip(sums, terms))
+
+    nothing = jnp.zeros((1, D), F32)
+    sums = lax.fori_loop(0, BLOCK // SUB, norm_part, (nothing,) * 4)
+    R.sg[3:4, :] = sums[0]
+    R.sg[4:5, :] = sums[1]
+    R.sg[2:3, :] = sums[2]
+    R.sg[5:6, :] = sums[3]
+
+    def dob_copy(d):
+        return z_copy(1, d, R.dobs.at[d - 1], R.dob.at[mine_rows, :])
+
+    for d in (3, 2, 1, 0):
+        part = nt(R.dxf[mine_rows, :], R.wof[tile(zx[d], 256), :]).astype(BF)
+        if d:
+            R.dobs[d - 1] = part
+            post(dob_copy(d))
+        else:
+            R.dob[mine_rows, :] = part
+
+    def z_spread(x, d, ref, source):
+        part = ref.at[rows32(zx[source] * BLOCK, BLOCK), :]
+        return z_copy(x, d, part, part)
+
+    for d in (3, 2, 1):
+        post(z_spread(2, d, R.dxf, 0))
+    for d in (3, 2, 1):
+        post(z_scatter(3, d, R.r2s, R.r2r))
+
+    for d in (1, 2, 3):
+        z_copy(1, d, R.dobs.at[d - 1], R.dob.at[rows32(zx[d] * BLOCK, BLOCK), :]).wait_recv()
+    R.dk[...] = jnp.zeros_like(R.dk)
+    R.dv[...] = jnp.zeros_like(R.dv)
+    down_bias = R.vecb[5:6, :]
+
+    @pl.loop(0, ROWS // LANES)
+    def _(b):
+        cols = tile(b, LANES)
+        query = R.qkv[0, cols, :]
+        grad = R.dob[cols, :]
+        for h in range(4):
+            lanes = slice(h * LANES, (h + 1) * LANES)
+            qm = only_head(query, h)
+            dm = only_head(grad, h)
+            R.qm4[lanes, :] = qm
+            R.dm4[lanes, :] = dm
+            p = jnp.exp(masked_scores(qm) - R.lse[h, :, cols])
+            R.p4[:, lanes] = p.astype(BF)
+            dp = nt(R.qkv[2], dm)
+            ds = (p * (dp - jnp.sum(p * dp, axis=0, keepdims=True))).astype(BF)
+            R.ds4[:, lanes] = ds
+            R.dqt[h * HEAD : (h + 1) * HEAD, :] = nn(R.kt[h * HEAD : (h + 1) * HEAD, :], ds)
+        R.dqkv[0, cols, :] = (R.dqt[...].T * HEAD ** (-0.5)).astype(BF)
+        R.dk[...] += nn(R.ds4[...], R.qm4[...])
+        R.dv[...] += nn(R.p4[...], R.dm4[...])
+
+    R.dqkv[1] = R.dk[...].astype(BF)
+    R.dqkv[2] = R.dv[...].astype(BF)
+
+    for d in (1, 2, 3):
+        z_scatter(3, d, R.r2s, R.r2r).wait_recv()
+
+    @pl.loop(0, BLOCK // SUB)
+    def _(i):
+        local = tile(i, SUB)
+        rows = rows32(mine + i * SUB, SUB)
+        y = (
+            R.x1[rows, :]
+            + R.du[rows32(BLOCK + i * SUB, SUB), :]
+            + R.r2r[0, local, :].astype(F32)
+            + R.r2r[1, local, :].astype(F32)
+            + R.r2r[2, local, :].astype(F32)
+            + down_bias
+        )
+        R.yb[rows, :] = y.astype(BF)
+
+    for c in range(3):
+        R.gwq[c] = nn(R.a1t[...], R.dqkv[c]).astype(BF)
+    pair_send("q")
+    R.sg[7:8, :] = jnp.concatenate(
+        [
+            jnp.sum(R.dqkv[0].astype(F32), axis=0, keepdims=True),
+            jnp.sum(R.dqkv[2].astype(F32), axis=0, keepdims=True),
+            jnp.zeros((1, 512), F32),
+        ],
+        axis=1,
+    )
+    R.sg[0:2, :] = jnp.zeros((2, D), F32)
+    for d in (3, 2, 1, 0):
+        start = zx[d] * BLOCK
+        rows = rows32(start, BLOCK)
+
+        @pl.loop(0, 4)
+        def _(n):
+            cols = tile(n, 256)
+            R.du[0:BLOCK, cols] = (
+                nt(R.dqkv[0, rows, :], R.wqkv[0, cols, :])
+                + nt(R.dqkv[1, rows, :], R.wqkv[1, cols, :])
+                + nt(R.dqkv[2, rows, :], R.wqkv[2, cols, :])
+            )
+
+        def first_part(i, sums):
+            local = tile(i, SUB)
+            dxn = R.du[local, :]
+            hat, _ = center_scale(R.xs[rows32(start + i * SUB, SUB), :].astype(F32))
+            if d:
+                R.r4s[d - 1, local, :] = dxn.astype(BF)
+            terms = (dxn * hat, dxn)
+            return tuple(s + jnp.sum(t, axis=0, keepdims=True) for s, t in zip(sums, terms))
+
+        sums = lax.fori_loop(0, BLOCK // SUB, first_part, (nothing,) * 2)
+        R.sg[0:1, :] += sums[0]
+        R.sg[1:2, :] += sums[1]
+
+    for d in (3, 2, 1):
+        post(z_copy(7, d, R.sg, R.sgz.at[d - 1]))
+    for d in (3, 2, 1):
+        post(z_scatter(5, d, R.r4s, R.r4r))
+    for d in (3, 2, 1):
+        post(z_spread(4, d, R.yb, 0))
+    pair_sum("q")
+    for d in (1, 2, 3):
+        z_spread(2, d, R.dxf, d).wait_recv()
+    R.gwo[...] = nn(R.ot[...], R.dxf[...]).astype(BF)
+    pair_send("o")
+    squares = cross_sum("r")
+    squares += cross_sum("e")
+    pair_sum("o")
+
+    for d in (1, 2, 3):
+        z_copy(7, d, R.sg, R.sgz.at[d - 1]).wait_recv()
+    shared_row = lax.broadcasted_iota(jnp.int32, (8, D), 0) < 6
+    others = R.sgz[0] + R.sgz[1] + R.sgz[2]
+    R.sgt[...] = R.sg[...] + jnp.where(shared_row, others, 0.0)
+
+    def d_copy(x, e, src, dst):
+        return remote(src, dst, R.d_s.at[x, e - 1], R.d_r.at[x, e - 1], {"dp": dpx[e]})
+
+    for e in (6, 7, 2, 3, 4, 5, 1):
+        post(d_copy(0, e, R.sgt, R.sgd.at[e - 1]))
+
+    for d in (1, 2, 3):
+        z_scatter(5, d, R.r4s, R.r4r).wait_recv()
+
+    @pl.loop(0, BLOCK // SUB)
+    def _(i):
+        local = tile(i, SUB)
+        rows = rows32(mine + i * SUB, SUB)
+        dxn = (
+            R.du[local, :]
+            + R.r4r[0, local, :].astype(F32)
+            + R.r4r[1, local, :].astype(F32)
+            + R.r4r[2, local, :].astype(F32)
+        )
+        hat, r = center_scale(R.xs[rows, :].astype(F32))
+        e = dxn * gain1
+        dx = R.du[rows32(3 * BLOCK + i * SUB, SUB), :] + r * (
+            e
+            - jnp.mean(e, axis=-1, keepdims=True)
+            - hat * jnp.mean(e * hat, axis=-1, keepdims=True)
+        )
+        R.xg[rows, :] = dx.astype(BF)
+
+    for d in (3, 2, 1):
+        post(z_spread(6, d, R.xg, 0))
+
+    squares += cross_sum("q")
+    squares += cross_sum("o")
+    for e in range(1, 8):
+        d_copy(0, e, R.sgt, R.sgd.at[e - 1]).wait_recv()
+    sg = R.sgt[...]
+    for e in range(1, 8):
+        sg = sg + R.sgd[e - 1]
+    R.sg_out[...] = sg
+    squared = sg * sg
+    shared_squares = jnp.sum(jnp.where(shared_row, squared, 0.0))
+    local_squares = jnp.sum(jnp.where(shared_row, 0.0, squared))
+    R.nrm[0] = jnp.full((8, LANES), squares + local_squares * 0.125, F32)
+    for e in (6, 7, 2, 3, 4, 5, 1):
+        post(d_copy(1, e, R.nrm.at[0], R.nrd.at[e - 1]))
+    for e in range(1, 8):
+        d_copy(1, e, R.nrm.at[0], R.nrd.at[e - 1]).wait_recv()
+    value = R.nrm[0]
+    for e in range(1, 8):
+        value = value + R.nrd[e - 1]
+    R.nrm[1] = value
+    for d in (3, 2, 1):
+        post(z_copy(8, d, R.nrm.at[1], R.nrz.at[d - 1]))
+
+    for d in (1, 2, 3):
+        z_spread(4, d, R.yb, d).wait_recv()
+    y_store = pltpu.make_async_copy(R.yb, R.y_out, R.ld.at[0])
+    y_store.start()
+    for d in (1, 2, 3):
+        z_spread(6, d, R.xg, d).wait_recv()
+    x_store = pltpu.make_async_copy(R.xg, R.xg_out, R.ld.at[1])
+    x_store.start()
+    for d in (1, 2, 3):
+        z_copy(8, d, R.nrm.at[1], R.nrz.at[d - 1]).wait_recv()
+    R.total[...] = R.nrm[1] + R.nrz[0] + R.nrz[1] + R.nrz[2] + shared_squares
+    for copy in sent:
+        copy.wait_send()
+
+    @pl.loop(0, ROWS // LANES)
+    def _(b):
+        for d in (1, 2, 3):
+            o_copy(b, d, 0).wait_send()
+
+    y_store.wait()
+    x_store.wait()
+
+
+def run_block(tokens, x_rows, gy_rows, small, triple, out, up, down):
+    kernel = functools.partial(block_kernel, tokens)
+    vmem = pl.BlockSpec(memory_space=pltpu.VMEM)
+    anywhere = pl.BlockSpec(memory_space=pl.ANY)
+    return pl.pallas_call(
+        kernel,
+        out_shape=(
+            jax.ShapeDtypeStruct((3, LANES, 256), F32),
+            jax.ShapeDtypeStruct((256, LANES), F32),
+            jax.ShapeDtypeStruct((LANES, D), F32),
+            jax.ShapeDtypeStruct((D, LANES), F32),
+            jax.ShapeDtypeStruct((8, D), F32),
+            jax.ShapeDtypeStruct((8, LANES), F32),
+            jax.ShapeDtypeStruct((ROWS, D), BF),
+            jax.ShapeDtypeStruct((ROWS, D), BF),
+        ),
+        in_specs=[anywhere] * len(INPUTS),
+        out_specs=(vmem,) * 6 + (anywhere,) * 2,
+        scratch_shapes=[
+            *(pltpu.VMEM(shape, dtype) for shape, dtype in SCRATCH.values()),
+            *(pltpu.SemaphoreType.DMA(shape) for shape in SEMS.values()),
+        ],
+        compiler_params=pltpu.CompilerParams(
+            collective_id=0, has_side_effects=True, vmem_limit_bytes=63 * 1024 * 1024
+        ),
+        name="block_step",
+    )(x_rows, gy_rows, small, triple, out, up, down)
+
+
+def fused_device(*args):
+    images, valid_flags, cotangent = args[:3]
+    masters, means, squares = args[3:15], args[15:27], args[27:39]
+    tokens = images.shape[1]
+    pad = ((0, ROWS - tokens), (0, 0))
+    x_rows = jnp.pad(images[0], pad)
+    gy_rows = jnp.pad(cotangent[0] * valid_flags[0].astype(BF), pad)
+    vectors = [masters[i].reshape(1, LANES) for i in (0, 1, 5, 6, 7, 11)]
+    small = jnp.concatenate(
+        [
+            *vectors,
+            masters[9].reshape(1, LANES),
+            jnp.pad(masters[3].reshape(1, HEAD), ((0, 0), (0, LANES - HEAD))),
+        ],
+        axis=0,
+    )
+    gq, go, ge, gr, sg, total, y_rows, grad_rows = run_block(
+        tokens, x_rows, gy_rows, small, masters[2], masters[4], masters[8], masters[10]
+    )
+    position = lax.axis_index("dp")
+    owned = lax.dynamic_slice_in_dim(sg[:6], position * LANES, LANES, 1)
+    expand = lax.dynamic_slice_in_dim(sg[6].reshape(16, 64), position * 8, 8, 1)
+    pairs = lax.dynamic_slice_in_dim(sg[7, :512].reshape(2, 4, 64), position * 8, 8, 2)
+    grads = (
+        owned[0], owned[1], gq, pairs, go, owned[2], owned[3], owned[4], ge, expand, gr, owned[5],
+    )
+    norm_value = jnp.sqrt(total[0, 0])
+    limit = math.sqrt(4 * D * D + 2 * D * FF + 8 * D + FF)
+    factor = jnp.minimum(1.0, limit / (norm_value + 1e-06))
+    updates = []
+    for master, row_mean, square, gradient, rate in zip(masters, means, squares, grads, rates):
+        updates.extend(adam_step(master, row_mean, square, gradient * factor, rate))
+    return (
+        y_rows[:tokens].reshape(images.shape),
+        grad_rows[:tokens].astype(F32).reshape(images.shape),
+        norm_value,
+        *updates,
+    )
+
+
 def solution(mesh):
     in_specs = (
         P("dp", None, None),
@@ -440,6 +1206,7 @@
         P("dp"),
         P("dp"),
     )
+    fused = mesh.shape["dp"] == 8 and mesh.shape["tensor"] == 4
     return jax.shard_map(
-        per_device, mesh=mesh, in_specs=in_specs, out_specs=out_specs, check_vma=False
-    )
+        fused_device if fused else per_device, mesh=mesh, in_specs=in_specs, out_specs=out_specs, check_vma=False
+    )

time: 785 us -> 284 us (0.36)
  waiting for transfers between devices: 482 us -> 0 us
  Pallas kernels: 0 us -> 250 us
  blocking collectives: 118 us -> 0 us
  matrix products: 66.1 us -> 0 us
  other arithmetic: 57.7 us -> 12.9 us
  between operations: 25.8 us -> 3.63 us
  local copies, waits for them, and re-layouts: 27 us -> 15 us
    psum x4 -> x0, waiting for transfers between devices: 436 us -> none  [the longest x1 152 us: per_device(): lax.psum(mlp_part, 'tensor')]
    pallas_call x0 -> x1, Pallas kernels: none -> 250 us  [run_block(): pl.pallas_call(kernel, out_shape=(jax.ShapeDtypeStruct((3, LANES, 256), F...]
    all_gather x9 -> x0, blocking collectives: 79.4 us -> none  [the longest x1 10.3 us: per_device(): lax.all_gather(rounded[1], 'dp', axis=0, tiled=True)]
    dot_general x18 -> x0, matrix products: 66.1 us -> none  [the longest x3 11.4 us: contract_rows(): lax.dot_general(left, right, (((0,), (0,)), ((), ())), preferred_element_...]
    all_gather x3 -> x0, waiting for transfers between devices: 46.7 us -> none  [the longest x1 26.4 us: per_device(): lax.all_gather(rounded[8], 'dp', axis=0, tiled=True)]
    psum x2 -> x0, blocking collectives: 38.7 us -> none  [the longest x1 26.6 us: per_device(): lax.psum((grads[0], grads[1], grads[2], grads[3], grads[4], grads[5], gra...]
    reduce_sum x21 -> x0, other arithmetic: 26.7 us -> none  [the longest x12 13.9 us: squared_total(): total = total + weight * jnp.sum(incoming_gradient * incoming_gradient)]
    unnamed x126 -> x83, local copies, waits for them, and re-layouts: 20.7 us -> 6.77 us
  transfers between devices with their start and end apart: 7 -> 0, of which waited for: 6 -> 0; matrix products, arithmetic and copies ran while one was open for 7% -> 0% of each run, Pallas kernels for 0% -> 0%
where the time goes in v1:
time: 284 us; the launch traced here: 281 us
  Pallas kernels  250 us (88%)
  local copies, waits for them, and re-layouts  15 us (5%)
  other arithmetic  12.9 us (5%)
  between operations  3.63 us (1%)
    pallas_call x1, Pallas kernels, run_block(): pl.pallas_call(kernel, out_shape=(jax.ShapeDtypeStruct((3, LANES, 256), F...  250 us
    convert_element_type x8, other arithmetic, adam_step(): return [updated, mean_new, square_new, updated.astype(jnp.bfloat16)]  8.49 us
    unnamed x83, local copies, waits for them, and re-layouts  6.77 us

profile of v1, /device:TPU:0, one launch (start us, length us, event | category | flops | bytes accessed | tf_op | source)
XLA Modules:
  0.0 281.4 jit_solution(6710021204329826731)
XLA Ops:
  1.4 0.8 reshape.158
  2.1 0.8 copy.93
  3.0 1.3 concatenate.3.refs_2_
  4.3 1.4 multiply_bitcast_fusion
  5.7 1.2 pad.12.refs_1_
  6.9 0.5 copy-done.3
  7.5 1.2 pad.11.refs_0_
  8.9 249.9 %block_step.1 = (f32[3,128,256]{2,1,0:T(8,128)}, f32[256,128]{1,0:T(8,128)}, f32[128,1024]{1,0:T(8,128)}, f32[1024,128]{1,0:T(8,128)}, f32[8,1024]{1,0:T(8,128)}...) custom-call(bf16[640,1024]{1,0:T(8,128)(2,1)} %pad.11.refs_0_, ...), custom_call_target="tpu_custom_call" | custom-call | tf_op jit(solution)/shard_map/block_step/pallas_call | solution.py:1049
  258.9 1.2 slice.38
  260.8 0.7 slice_reduce_fusion.1
  261.6 0.7 constant_dynamic-slice_fusion.1
  262.3 0.8 slice_reduce_fusion
  263.3 0.6 fusion.32
  264.0 0.6 fusion.12
  264.6 0.7 fusion.28
  265.3 0.6 fusion.16
  266.0 1.7 fusion.26
  267.7 3.0 %bitcast_convert_fusion = (f32[1,577,1024]{2,1,0:T(8,128)S(1)}, bf16[1,577,1024]{2,1,0:T(8,128)(2,1)}) fusion(bf16[640,1024]{1,0:T(8,128)(2,1)} %get-tuple-element.60, bf16[640,1024]{1,0:T(8,128)(2,1)} %get-tuple-element.59), kind=kLoop, calls=%fused_computation | loop fusion | flops 590848 | bytes 5908480 | tf_op jit(solution)/shard_map/reshape | solution.py:1108
  270.7 3.8 %copy.95 = f32[1,577,1024]{2,0,1:T(1,128)} copy(f32[1,577,1024]{2,1,0:T(8,128)S(1)} %get-tuple-element.233) | data formatting | bytes 4726784
  274.6 1.3 fusion.30
  276.1 0.3 copy-done.5
  276.6 1.5 fusion.14
  278.1 0.5 copy-done.7
  278.8 1.5 fusion.18
  (83 shorter events, 1.1 us)
Async XLA Ops:
  8.6 254.7 %copy-start.29 = (f32[128]{0:T(128)S(1)}, f32[128]{0:T(128)}, u32[]{:S(2)}) copy-start(f32[128]{0:T(128)} %param.55) | copy-start | bytes 1540
  8.6 254.7 %copy-start.30 = (f32[128]{0:T(128)S(1)}, f32[128]{0:T(128)}, u32[]{:S(2)}) copy-start(f32[128]{0:T(128)} %param.66) | copy-start | bytes 1540
  8.6 254.7 %copy-start.31 = (f32[128]{0:T(128)S(1)}, f32[128]{0:T(128)}, u32[]{:S(2)}) copy-start(f32[128]{0:T(128)} %param.54) | copy-start | bytes 1540
  8.7 255.2 %copy-start.24 = (f32[128]{0:T(128)S(1)}, f32[128]{0:T(128)}, u32[]{:S(2)}) copy-start(f32[128]{0:T(128)} %param.47) | copy-start | bytes 1540
  8.7 255.2 %copy-start.25 = (f32[128]{0:T(128)S(1)}, f32[128]{0:T(128)}, u32[]{:S(2)}) copy-start(f32[128]{0:T(128)} %param.48) | copy-start | bytes 1540
  8.7 255.2 %copy-start.26 = (f32[128]{0:T(128)S(1)}, f32[128]{0:T(128)}, u32[]{:S(2)}) copy-start(f32[128]{0:T(128)} %param.49) | copy-start | bytes 1540
  8.7 255.2 %copy-start.27 = (f32[128]{0:T(128)S(1)}, f32[128]{0:T(128)}, u32[]{:S(2)}) copy-start(f32[128]{0:T(128)} %param.53) | copy-start | bytes 1540
  8.7 255.2 %copy-start.32 = (f32[128]{0:T(128)S(1)}, f32[128]{0:T(128)}, u32[]{:S(2)}) copy-start(f32[128]{0:T(128)} %param.77) | copy-start | bytes 1540
  8.7 255.2 %copy-start.33 = (f32[128]{0:T(128)S(1)}, f32[128]{0:T(128)}, u32[]{:S(2)}) copy-start(f32[128]{0:T(128)} %param.65) | copy-start | bytes 1540
  8.7 255.2 %copy-start.34 = (f32[128]{0:T(128)S(1)}, f32[128]{0:T(128)}, u32[]{:S(2)}) copy-start(f32[128]{0:T(128)} %param.73) | copy-start | bytes 1540
  8.7 255.2 %copy-start.35 = (f32[128]{0:T(128)S(1)}, f32[128]{0:T(128)}, u32[]{:S(2)}) copy-start(f32[128]{0:T(128)} %param.61) | copy-start | bytes 1540
  8.8 255.2 %copy-start.36 = (f32[128]{0:T(128)S(1)}, f32[128]{0:T(128)}, u32[]{:S(2)}) copy-start(f32[128]{0:T(128)} %param.72) | copy-start | bytes 1540
  8.8 255.2 %copy-start.37 = (f32[128]{0:T(128)S(1)}, f32[128]{0:T(128)}, u32[]{:S(2)}) copy-start(f32[128]{0:T(128)} %param.60) | copy-start | bytes 1540
  8.8 255.2 %copy-start.38 = (f32[128]{0:T(128)S(1)}, f32[128]{0:T(128)}, u32[]{:S(2)}) copy-start(f32[128]{0:T(128)} %param.71) | copy-start | bytes 1540
  8.8 255.2 %copy-start.39 = (f32[128]{0:T(128)S(1)}, f32[128]{0:T(128)}, u32[]{:S(2)}) copy-start(f32[128]{0:T(128)} %param.59) | copy-start | bytes 1540
  8.8 255.8 %copy-start.17 = (f32[2,4,8]{2,1,0:T(4,128)S(1)}, f32[2,4,8]{2,1,0:T(4,128)}, u32[]{:S(2)}) copy-start(f32[2,4,8]{2,1,0:T(4,128)} %param.45) | copy-start | bytes 772
  8.8 255.8 %copy-start.20 = (f32[2,4,8]{2,1,0:T(4,128)S(1)}, f32[2,4,8]{2,1,0:T(4,128)}, u32[]{:S(2)}) copy-start(f32[2,4,8]{2,1,0:T(4,128)} %param.69) | copy-start | bytes 772
  8.8 255.8 %copy-start.21 = (f32[2,4,8]{2,1,0:T(4,128)S(1)}, f32[2,4,8]{2,1,0:T(4,128)}, u32[]{:S(2)}) copy-start(f32[2,4,8]{2,1,0:T(4,128)} %param.57) | copy-start | bytes 772
  8.8 256.5 %copy-start.16 = (f32[16,8]{0,1:T(8,128)S(1)}, f32[16,8]{0,1:T(8,128)}, u32[]{:S(2)}) copy-start(f32[16,8]{0,1:T(8,128)} %param.51) | copy-start | bytes 1540
  8.9 256.5 %copy-start.18 = (f32[16,8]{0,1:T(8,128)S(1)}, f32[16,8]{0,1:T(8,128)}, u32[]{:S(2)}) copy-start(f32[16,8]{0,1:T(8,128)} %param.75) | copy-start | bytes 1540
  8.9 256.5 %copy-start.19 = (f32[16,8]{0,1:T(8,128)S(1)}, f32[16,8]{0,1:T(8,128)}, u32[]{:S(2)}) copy-start(f32[16,8]{0,1:T(8,128)} %param.63) | copy-start | bytes 1540
  8.9 257.1 %copy-start.10 = (f32[256,128]{1,0:T(8,128)S(1)}, f32[256,128]{1,0:T(8,128)}, u32[]{:S(2)}) copy-start(f32[256,128]{1,0:T(8,128)} %refs_4_.1) | copy-start | bytes 393220
  8.9 257.1 %copy-start.14 = (f32[256,128]{1,0:T(8,128)S(1)}, f32[256,128]{1,0:T(8,128)}, u32[]{:S(2)}) copy-start(f32[256,128]{1,0:T(8,128)} %param.70) | copy-start | bytes 393220
  8.9 257.1 %copy-start.15 = (f32[256,128]{1,0:T(8,128)S(1)}, f32[256,128]{1,0:T(8,128)}, u32[]{:S(2)}) copy-start(f32[256,128]{1,0:T(8,128)} %param.58) | copy-start | bytes 393220
  (16 other events, 794.9 us)

commit v2 on v1

--- a/solution.py
+++ b/solution.py
@@ -378,10 +378,14 @@
 
 
 def tile(index, size):
+    if isinstance(index, int):
+        return pl.ds(index * size, size)
     return pl.ds(pl.multiple_of(index * size, size), size)
 
 
 def rows32(start, size):
+    if isinstance(start, int):
+        return pl.ds(start, size)
     return pl.ds(pl.multiple_of(start, SUB), size)
 
 
@@ -418,13 +422,11 @@
     hb=((ROWS, 256), F32),
     u=((ROWS, D), BF),
     dhb=((ROWS, D), BF),
-    r3s=((3, BLOCK, D), BF),
-    r3r=((3, BLOCK, D), BF),
-    r2s=((3, BLOCK, D), BF),
-    r2r=((3, BLOCK, D), BF),
-    r4s=((3, BLOCK, D), BF),
-    r4r=((3, BLOCK, D), BF),
-    dxf=((ROWS, D), BF),
+    rs=((3, 3, BLOCK, D), BF),
+    rout=((3, 3, BLOCK, D), BF),
+    rin=((3, 2, BLOCK, D), BF),
+    dxb=((256, D), BF),
+    ott=((D, 256), BF),
     dobs=((3, BLOCK, 256), BF),
     dob=((ROWS, 256), BF),
     ds4=((ROWS, 512), BF),
@@ -439,15 +441,18 @@
     xg=((ROWS, D), BF),
     gwr=((D, D), BF),
     gwe=((D, D), BF),
-    gwo=((256, D), BF),
+    gwo=((D, D), BF),
     gwq=((3, D, 256), BF),
     pr_r=((4, D, LANES), BF),
     pr_e=((4, LANES, D), BF),
-    pr_o=((4, 256, LANES), BF),
+    pr_o=((4, D, LANES), BF),
     pr_q=((4, 3, LANES, 256), BF),
     cr_r=((3, D, LANES), BF),
     cr_e=((3, LANES, D), BF),
-    cr_o=((3, 256, LANES), BF),
+    cr_o=((3, D, LANES), BF),
+    go_sum=((D, LANES), F32),
+    goz=((D, LANES), BF),
+    gor=((3, 256, LANES), BF),
     cr_q=((3, 3, LANES, 256), BF),
     sg=((8, D), F32),
     sgz=((3, 8, D), F32),
@@ -463,10 +468,15 @@
     g_r=(5, 8),
     wz_s=(3,),
     wz_r=(3,),
-    o_s=(5, 3),
-    o_r=(5, 3),
-    z_s=(9, 3),
-    z_r=(9, 3),
+    o_s=(5, 5),
+    o_r=(5, 4),
+    z_s=(4, 3),
+    z_r=(4, 3),
+    rs_s=(3, 3),
+    ro_r=(3, 3),
+    ri_r=(3, 2),
+    ag_s=(2, 5),
+    ag_r=(2, 4),
     p_s=(4, 4),
     p_r=(4, 4),
     c_s=(4, 3),
@@ -485,6 +495,17 @@
     z = lax.axis_index("tensor")
     dpx = [flip(me, e, 3) for e in range(8)]
     zx = [flip(z, d, 2) for d in range(4)]
+    half = lax.div(z, 2)
+    near = z + half * (3 - 2 * z)
+    inner = z + 1 - 2 * half
+    outer = z - 1 + 2 * half
+    at_end = near == 0
+    at_middle = near == 1
+
+    def seen(j):
+        return j + half * (3 - 2 * j)
+
+    order = (seen(3), seen(2), seen(1 - near), z)
     sent = []
 
     def remote(src, dst, send, recv, where):
@@ -527,23 +548,163 @@
         "e": (4, lambda j: R.we.at[tile(j, LANES), :]),
     }
 
-    def gather_copy(name, source, target, slot):
+    HALF = {
+        "o": lambda j, part: R.wof.at[tile(part, D // 2), tile(j, LANES)],
+        "r": lambda j, part: R.wr.at[tile(part, D // 2), tile(j, LANES)],
+        "e": lambda j, part: R.we.at[tile(2 * j + part, LANES // 2), :],
+    }
+
+    def gather_copy(name, source, target, slot, part=None):
         a, region = GATHER[name]
-        part = region(dpx[source])
-        return remote(part, part, R.g_s.at[a, slot], R.g_r.at[a, slot], {"dp": dpx[target]})
-
-    def gather_send(name):
-        for e in (6, 2, 4, 1):
-            post(gather_copy(name, 0, e, e))
+        piece = region(dpx[source]) if part is None else HALF[name](dpx[source], part)
+        return remote(piece, piece, R.g_s.at[a, slot], R.g_r.at[a, slot], {"dp": dpx[target]})
+
+    gathered = []
+
+    def gather_post(*where):
+        gather_copy(*where).start()
+        gathered.append(where)
+
+    def gather_send(name, targets=(6, 2, 4, 1)):
+        for e in targets:
+            gather_post(name, 0, e, e)
 
     def gather_pass(name):
         for e in (2, 4, 6):
             gather_copy(name, e, e, e).wait_recv()
-            post(gather_copy(name, e, 1, e + 1))
+            gather_post(name, e, 1, e + 1)
+
+    def gather_relay(name):
+        gather_copy(name, 2, 2, 2).wait_recv()
+        gather_post(name, 2, 4, 6, 0)
+        gather_copy(name, 4, 4, 4).wait_recv()
+        gather_post(name, 4, 2, 0, 1)
+        gather_post(name, 2, 1, 3)
+        gather_post(name, 4, 1, 5)
+
+    def gather_last(name):
+        gather_copy(name, 6, 4, 6, 0).wait_recv()
+        gather_copy(name, 6, 2, 0, 1).wait_recv()
+        gather_post(name, 6, 1, 7)
 
     def gather_wait(name):
         for e in (1, 3, 5, 7):
             gather_copy(name, e, 1, e).wait_recv()
+
+    def to_inner(src, dst, send, recv):
+        return remote(src, dst, send, recv, {"tensor": inner})
+
+    def to_outer(src, dst, send, recv):
+        return remote(src, dst, send, recv, {"tensor": outer})
+
+    def add_into(x, k, other, slot):
+        @pl.loop(0, BLOCK // SUB)
+        def _(i):
+            rows = tile(i, SUB)
+            total = R.rs[x, k, rows, :].astype(F32) + other[x, slot, rows, :].astype(F32)
+            R.rs[x, k, rows, :] = total.astype(BF)
+
+    class Scatter:
+        def __init__(self, x):
+            self.x = x
+
+        def inward(self, k, dst, recv):
+            return to_inner(R.rs.at[self.x, k], dst, R.rs_s.at[self.x, k], recv)
+
+        def from_end(self, k):
+            return self.inward(k, R.rout.at[self.x, k], R.ro_r.at[self.x, k])
+
+        def across(self, k):
+            return self.inward(k, R.rin.at[self.x, k], R.ri_r.at[self.x, k])
+
+        def outward(self):
+            return to_outer(
+                R.rs.at[self.x, 2], R.rin.at[self.x, 0], R.rs_s.at[self.x, 2], R.ri_r.at[self.x, 0]
+            )
+
+        def end(self, k):
+            @pl.when(at_end)
+            def _():
+                self.from_end(k).start()
+
+        def step(self, k):
+            @pl.when(at_middle)
+            def _():
+                if k < 2:
+                    self.from_end(k).wait_recv()
+                    add_into(self.x, k, R.rout, k)
+                    self.across(k).start()
+                else:
+                    self.across(0).wait_recv()
+                    add_into(self.x, 2, R.rin, 0)
+                    self.outward().start()
+
+        def finish(self, add):
+            @pl.when(at_middle)
+            def _():
+                self.from_end(2).wait_recv()
+                add(R.rout, self.x, 2)
+                self.across(1).wait_recv()
+                add(R.rin, self.x, 1)
+
+            @pl.when(at_end)
+            def _():
+                self.across(0).wait_recv()
+                add(R.rin, self.x, 0)
+
+        def drain(self):
+            for k in range(3):
+                self.from_end(k).wait_send()
+
+    class Spread:
+        def __init__(self, region, sends, recvs, x):
+            self.region, self.sends, self.recvs, self.x = region, sends, recvs, x
+
+        def inward(self, j, slot, recv):
+            part = self.region(seen(j))
+            return to_inner(part, part, self.sends.at[self.x, slot], self.recvs.at[self.x, recv])
+
+        def outward(self, j, slot, recv):
+            part = self.region(seen(j))
+            return to_outer(part, part, self.sends.at[self.x, slot], self.recvs.at[self.x, recv])
+
+        def start(self):
+            @pl.when(at_end)
+            def _():
+                self.inward(0, 0, 0).start()
+
+            @pl.when(at_middle)
+            def _():
+                self.inward(1, 0, 2).start()
+                self.outward(1, 1, 1).start()
+
+        def first(self):
+            @pl.when(at_middle)
+            def _():
+                self.outward(0, 2, 0).wait_recv()
+                self.inward(0, 2, 3).start()
+                self.inward(2, 3, 2).wait_recv()
+                self.outward(2, 3, 2).start()
+
+        def second(self):
+            @pl.when(at_middle)
+            def _():
+                self.inward(3, 4, 3).wait_recv()
+                self.outward(3, 4, 3).start()
+
+        def finish(self):
+            @pl.when(at_end)
+            def _():
+                for j in (1, 2, 3):
+                    self.inward(j, 0, j).wait_recv()
+
+        def drain(self):
+            self.inward(0, 0, 0).wait_send()
+
+            @pl.when(at_middle)
+            def _():
+                for slot in (1, 2, 3, 4):
+                    self.inward(1, slot, 0).wait_send()
 
     own = tile(me, LANES)
     loads[0].wait()
@@ -565,9 +726,7 @@
     for d in (1, 2, 3):
         part = R.wof.at[tile(zx[d], 256), own]
         remote(part, part, R.wz_s.at[d - 1], R.wz_r.at[d - 1], {"tensor": zx[d]}).wait_recv()
-    gather_send("o")
-    gather_send("r")
-    gather_send("e")
+    gather_send("o", (2, 4, 1))
 
     gather_pass("small")
     gather_wait("small")
@@ -615,6 +774,7 @@
     flip_into(R.a1t, R.a1)
 
     gather_pass("q")
+    gather_send("r", (2, 4, 1))
     gather_wait("q")
 
     @pl.loop(0, 3)
@@ -637,9 +797,10 @@
     def only_head(value, h):
         return jnp.where(head_lane == h, value, jnp.zeros_like(value))
 
-    def o_copy(b, d, source):
-        part = R.of.at[tile(b, LANES), tile(zx[source], 256)]
-        return remote(part, part, R.o_s.at[b, d - 1], R.o_r.at[b, d - 1], {"tensor": zx[d]})
+    def o_spread(b):
+        return Spread(lambda j: R.of.at[tile(b, LANES), tile(j, 256)], R.o_s, R.o_r, b)
+
+    blocks = ROWS // LANES
 
     @pl.loop(0, ROWS // LANES)
     def _(b):
@@ -655,27 +816,36 @@
             mixed = nn(R.vt[h * HEAD : (h + 1) * HEAD, :], pb)
             R.ot[h * HEAD : (h + 1) * HEAD, cols] = mixed.astype(BF)
         R.of[cols, tile(z, 256)] = R.ot[:, cols].T
-        for d in (3, 2, 1):
-            o_copy(b, d, 0).start()
-
-    gather_pass("o")
+        o_spread(b).start()
+
+        @pl.when(b >= 1)
+        def _():
+            o_spread(b - 1).first()
+
+        @pl.when(b >= 2)
+        def _():
+            o_spread(b - 2).second()
+
+        @pl.when(b == 1)
+        def _():
+            gather_relay("o")
+            gather_send("e", (2, 4, 1))
+
+    o_spread(blocks - 1).first()
+    o_spread(blocks - 2).second()
     loads[6].wait()
-    gather_pass("r")
-    gather_wait("r")
-
-    @pl.loop(0, 4)
-    def _(n):
-        R.du[:, tile(n, 256)] = nt(R.gyb[...], R.wr[tile(n, 256), :])
-
+    gather_last("o")
+    gather_relay("r")
+    o_spread(blocks - 1).second()
     gather_wait("o")
+
     out_bias = R.vecb[2:3, :]
     gain2, shift2 = R.vecb[3:4, :], R.vecb[4:5, :]
 
     @pl.loop(0, ROWS // LANES)
     def _(b):
         rows = tile(b, LANES)
-        for d in (1, 2, 3):
-            o_copy(b, d, d).wait_recv()
+        o_spread(b).finish()
 
         @pl.loop(0, 4)
         def _(n):
@@ -690,7 +860,15 @@
             hat, _ = center_scale(v)
             R.a2[part, :] = (hat * gain2 + shift2).astype(BF)
 
-    gather_pass("e")
+    gather_last("r")
+    gather_relay("e")
+    gather_wait("r")
+
+    @pl.loop(0, 4)
+    def _(n):
+        R.du[:, tile(n, 256)] = nt(R.gyb[...], R.wr[tile(n, 256), :])
+
+    gather_last("e")
     gather_wait("e")
 
     @pl.loop(0, 4)
@@ -713,28 +891,26 @@
     def z_copy(x, d, src, dst):
         return remote(src, dst, R.z_s.at[x, d - 1], R.z_r.at[x, d - 1], {"tensor": zx[d]})
 
-    def z_scatter(x, d, s, r):
-        return z_copy(x, d, s.at[d - 1], r.at[d - 1])
-
-    for d in (3, 2, 1, 0):
-        rows = rows32(zx[d] * BLOCK, BLOCK)
+    scatter3, scatter2, scatter4 = Scatter(0), Scatter(1), Scatter(2)
+    for k in range(4):
+        rows = rows32(order[k] * BLOCK, BLOCK)
 
         @pl.loop(0, 4)
         def _(n):
             cols = tile(n, 256)
             part = nt(R.dhb[rows, :], R.we[cols, :])
-            if d:
-                R.r3s[d - 1, :, cols] = part.astype(BF)
+            if k < 3:
+                R.rs[0, k, :, cols] = part.astype(BF)
             else:
                 R.du[0:BLOCK, cols] = part
 
-        if d:
-            post(z_scatter(0, d, R.r3s, R.r3r))
+        if k < 3:
+            scatter3.end(k)
 
     PIECES = {
         "r": (0, R.pr_r, R.cr_r, R.gr, lambda j: R.gwr.at[:, tile(j, LANES)]),
         "e": (1, R.pr_e, R.cr_e, R.ge, lambda j: R.gwe.at[tile(j, LANES), :]),
-        "o": (2, R.pr_o, R.cr_o, R.go, lambda j: R.gwo.at[:, tile(j, LANES)]),
+        "o": (2, R.pr_o, R.cr_o, R.go_sum, lambda j: R.gwo.at[:, tile(j, LANES)]),
         "q": (3, R.pr_q, R.cr_q, R.gq, lambda j: R.gwq.at[:, tile(j, LANES), :]),
     }
 
@@ -789,36 +965,42 @@
         R.gwe[:, tile(n, 256)] = nn(R.tt[...], R.dhb[:, tile(n, 256)]).astype(BF)
 
     pair_send("e")
+    scatter3.step(0)
     pair_sum("r")
 
-    for d in (3, 2, 1, 0):
-        rows = rows32(zx[d] * BLOCK, BLOCK)
+    for k in range(4):
+        rows = rows32(order[k] * BLOCK, BLOCK)
 
         @pl.loop(0, 4)
         def _(n):
             cols = tile(n, 256)
             part = nn(R.u[rows, :], R.wr[:, cols])
-            if d:
-                R.r2s[d - 1, :, cols] = part.astype(BF)
+            if k < 3:
+                R.rs[1, k, :, cols] = part.astype(BF)
             else:
                 R.du[BLOCK : 2 * BLOCK, cols] = part
 
+    scatter3.step(1)
     pair_sum("e")
+    scatter3.step(2)
 
     mine = z * BLOCK
     mine_rows = rows32(mine, BLOCK)
-    for d in (1, 2, 3):
-        z_scatter(0, d, R.r3s, R.r3r).wait_recv()
+
+    def add_to(start):
+        def add(other, x, slot):
+            @pl.loop(0, BLOCK // SUB)
+            def _(i):
+                R.du[rows32(start + i * SUB, SUB), :] += other[x, slot, tile(i, SUB), :].astype(F32)
+
+        return add
+
+    scatter3.finish(add_to(0))
 
     def norm_part(i, sums):
         local = tile(i, SUB)
         rows = rows32(mine + i * SUB, SUB)
-        dxn = (
-            R.du[local, :]
-            + R.r3r[0, local, :].astype(F32)
-            + R.r3r[1, local, :].astype(F32)
-            + R.r3r[2, local, :].astype(F32)
-        )
+        dxn = R.du[local, :]
         hat, r = center_scale(R.x1[rows, :])
         gy = R.gyb[rows, :].astype(F32)
         e = dxn * gain2
@@ -828,7 +1010,7 @@
             - hat * jnp.mean(e * hat, axis=-1, keepdims=True)
         )
         R.du[rows32(3 * BLOCK + i * SUB, SUB), :] = dx
-        R.dxf[rows, :] = dx.astype(BF)
+        R.dxb[local, :] = dx.astype(BF)
         terms = (dxn * hat, dxn, dx, gy)
         return tuple(s + jnp.sum(t, axis=0, keepdims=True) for s, t in zip(sums, terms))
 
@@ -840,27 +1022,34 @@
     R.sg[5:6, :] = sums[3]
 
     def dob_copy(d):
-        return z_copy(1, d, R.dobs.at[d - 1], R.dob.at[mine_rows, :])
+        return z_copy(0, d, R.dobs.at[d - 1], R.dob.at[mine_rows, :])
 
     for d in (3, 2, 1, 0):
-        part = nt(R.dxf[mine_rows, :], R.wof[tile(zx[d], 256), :]).astype(BF)
+        part = nt(R.dxb[0:BLOCK, :], R.wof[tile(zx[d], 256), :]).astype(BF)
         if d:
             R.dobs[d - 1] = part
             post(dob_copy(d))
         else:
             R.dob[mine_rows, :] = part
 
-    def z_spread(x, d, ref, source):
-        part = ref.at[rows32(zx[source] * BLOCK, BLOCK), :]
-        return z_copy(x, d, part, part)
-
-    for d in (3, 2, 1):
-        post(z_spread(2, d, R.dxf, 0))
-    for d in (3, 2, 1):
-        post(z_scatter(3, d, R.r2s, R.r2r))
+    for k in range(3):
+        scatter2.end(k)
+
+    R.dxb[BLOCK:, :] = jnp.zeros((256 - BLOCK, D), BF)
+    R.ott[:, 128:] = jnp.zeros((D, 128), BF)
+
+    @pl.loop(0, D // LANES)
+    def _(i):
+        R.ott[tile(i, LANES), 0:BLOCK] = R.of[mine_rows, tile(i, LANES)].T
+
+    @pl.loop(0, 4)
+    def _(n):
+        R.gwo[:, tile(n, 256)] = nn(R.ott[...], R.dxb[:, tile(n, 256)]).astype(BF)
+
+    pair_send("o")
 
     for d in (1, 2, 3):
-        z_copy(1, d, R.dobs.at[d - 1], R.dob.at[rows32(zx[d] * BLOCK, BLOCK), :]).wait_recv()
+        z_copy(0, d, R.dobs.at[d - 1], R.dob.at[rows32(zx[d] * BLOCK, BLOCK), :]).wait_recv()
     R.dk[...] = jnp.zeros_like(R.dk)
     R.dv[...] = jnp.zeros_like(R.dv)
     down_bias = R.vecb[5:6, :]
@@ -889,26 +1078,9 @@
     R.dqkv[1] = R.dk[...].astype(BF)
     R.dqkv[2] = R.dv[...].astype(BF)
 
-    for d in (1, 2, 3):
-        z_scatter(3, d, R.r2s, R.r2r).wait_recv()
-
-    @pl.loop(0, BLOCK // SUB)
-    def _(i):
-        local = tile(i, SUB)
-        rows = rows32(mine + i * SUB, SUB)
-        y = (
-            R.x1[rows, :]
-            + R.du[rows32(BLOCK + i * SUB, SUB), :]
-            + R.r2r[0, local, :].astype(F32)
-            + R.r2r[1, local, :].astype(F32)
-            + R.r2r[2, local, :].astype(F32)
-            + down_bias
-        )
-        R.yb[rows, :] = y.astype(BF)
-
-    for c in range(3):
-        R.gwq[c] = nn(R.a1t[...], R.dqkv[c]).astype(BF)
-    pair_send("q")
+    for k in range(3):
+        scatter2.step(k)
+
     R.sg[7:8, :] = jnp.concatenate(
         [
             jnp.sum(R.dqkv[0].astype(F32), axis=0, keepdims=True),
@@ -918,8 +1090,8 @@
         axis=1,
     )
     R.sg[0:2, :] = jnp.zeros((2, D), F32)
-    for d in (3, 2, 1, 0):
-        start = zx[d] * BLOCK
+    for k in range(4):
+        start = order[k] * BLOCK
         rows = rows32(start, BLOCK)
 
         @pl.loop(0, 4)
@@ -935,32 +1107,53 @@
             local = tile(i, SUB)
             dxn = R.du[local, :]
             hat, _ = center_scale(R.xs[rows32(start + i * SUB, SUB), :].astype(F32))
-            if d:
-                R.r4s[d - 1, local, :] = dxn.astype(BF)
+            if k < 3:
+                R.rs[2, k, local, :] = dxn.astype(BF)
             terms = (dxn * hat, dxn)
             return tuple(s + jnp.sum(t, axis=0, keepdims=True) for s, t in zip(sums, terms))
 
         sums = lax.fori_loop(0, BLOCK // SUB, first_part, (nothing,) * 2)
         R.sg[0:1, :] += sums[0]
         R.sg[1:2, :] += sums[1]
+        if k < 3:
+            scatter4.end(k)
 
     for d in (3, 2, 1):
-        post(z_copy(7, d, R.sg, R.sgz.at[d - 1]))
-    for d in (3, 2, 1):
-        post(z_scatter(5, d, R.r4s, R.r4r))
-    for d in (3, 2, 1):
-        post(z_spread(4, d, R.yb, 0))
+        post(z_copy(1, d, R.sg, R.sgz.at[d - 1]))
+
+    @pl.loop(0, 3)
+    def _(c):
+        R.gwq[c] = nn(R.a1t[...], R.dqkv[c]).astype(BF)
+
+    pair_send("q")
+    pair_sum("o")
+    scatter4.step(0)
+
+    scatter2.finish(add_to(BLOCK))
+
+    @pl.loop(0, BLOCK // SUB)
+    def _(i):
+        rows = rows32(mine + i * SUB, SUB)
+        y = R.x1[rows, :] + R.du[rows32(BLOCK + i * SUB, SUB), :] + down_bias
+        R.yb[rows, :] = y.astype(BF)
+
+    y_spread = Spread(
+        lambda j: R.yb.at[rows32(j * BLOCK, BLOCK), :], R.ag_s, R.ag_r, 0
+    )
+    x_spread = Spread(
+        lambda j: R.xg.at[rows32(j * BLOCK, BLOCK), :], R.ag_s, R.ag_r, 1
+    )
+    y_spread.start()
     pair_sum("q")
+    scatter4.step(1)
+    squares = cross_sum("r")
+    y_spread.first()
+    scatter4.step(2)
+    squares += cross_sum("e")
+    y_spread.second()
+
     for d in (1, 2, 3):
-        z_spread(2, d, R.dxf, d).wait_recv()
-    R.gwo[...] = nn(R.ot[...], R.dxf[...]).astype(BF)
-    pair_send("o")
-    squares = cross_sum("r")
-    squares += cross_sum("e")
-    pair_sum("o")
-
-    for d in (1, 2, 3):
-        z_copy(7, d, R.sg, R.sgz.at[d - 1]).wait_recv()
+        z_copy(1, d, R.sg, R.sgz.at[d - 1]).wait_recv()
     shared_row = lax.broadcasted_iota(jnp.int32, (8, D), 0) < 6
     others = R.sgz[0] + R.sgz[1] + R.sgz[2]
     R.sgt[...] = R.sg[...] + jnp.where(shared_row, others, 0.0)
@@ -971,19 +1164,13 @@
     for e in (6, 7, 2, 3, 4, 5, 1):
         post(d_copy(0, e, R.sgt, R.sgd.at[e - 1]))
 
-    for d in (1, 2, 3):
-        z_scatter(5, d, R.r4s, R.r4r).wait_recv()
+    scatter4.finish(add_to(0))
 
     @pl.loop(0, BLOCK // SUB)
     def _(i):
         local = tile(i, SUB)
         rows = rows32(mine + i * SUB, SUB)
-        dxn = (
-            R.du[local, :]
-            + R.r4r[0, local, :].astype(F32)
-            + R.r4r[1, local, :].astype(F32)
-            + R.r4r[2, local, :].astype(F32)
-        )
+        dxn = R.du[local, :]
         hat, r = center_scale(R.xs[rows, :].astype(F32))
         e = dxn * gain1
         dx = R.du[rows32(3 * BLOCK + i * SUB, SUB), :] + r * (
@@ -993,13 +1180,27 @@
         )
         R.xg[rows, :] = dx.astype(BF)
 
+    x_spread.start()
+
+    cross_sum("o")
+    R.goz[...] = R.go_sum[...].astype(BF)
     for d in (3, 2, 1):
-        post(z_spread(6, d, R.xg, 0))
-
+        post(z_copy(3, d, R.goz.at[tile(zx[d], 256), :], R.gor.at[d - 1]))
     squares += cross_sum("q")
-    squares += cross_sum("o")
+    x_spread.first()
     for e in range(1, 8):
         d_copy(0, e, R.sgt, R.sgd.at[e - 1]).wait_recv()
+    x_spread.second()
+    for d in (1, 2, 3):
+        z_copy(3, d, R.goz.at[tile(zx[d], 256), :], R.gor.at[d - 1]).wait_recv()
+    own_out = (
+        R.go_sum[tile(z, 256), :]
+        + R.gor[0].astype(F32)
+        + R.gor[1].astype(F32)
+        + R.gor[2].astype(F32)
+    )
+    R.go[...] = own_out
+    squares += jnp.sum(own_out * own_out)
     sg = R.sgt[...]
     for e in range(1, 8):
         sg = sg + R.sgd[e - 1]
@@ -1017,26 +1218,28 @@
         value = value + R.nrd[e - 1]
     R.nrm[1] = value
     for d in (3, 2, 1):
-        post(z_copy(8, d, R.nrm.at[1], R.nrz.at[d - 1]))
-
-    for d in (1, 2, 3):
-        z_spread(4, d, R.yb, d).wait_recv()
+        post(z_copy(2, d, R.nrm.at[1], R.nrz.at[d - 1]))
+
+    y_spread.finish()
     y_store = pltpu.make_async_copy(R.yb, R.y_out, R.ld.at[0])
     y_store.start()
-    for d in (1, 2, 3):
-        z_spread(6, d, R.xg, d).wait_recv()
+    x_spread.finish()
     x_store = pltpu.make_async_copy(R.xg, R.xg_out, R.ld.at[1])
     x_store.start()
     for d in (1, 2, 3):
-        z_copy(8, d, R.nrm.at[1], R.nrz.at[d - 1]).wait_recv()
+        z_copy(2, d, R.nrm.at[1], R.nrz.at[d - 1]).wait_recv()
     R.total[...] = R.nrm[1] + R.nrz[0] + R.nrz[1] + R.nrz[2] + shared_squares
     for copy in sent:
         copy.wait_send()
+    for where in gathered:
+        gather_copy(*where).wait_send()
 
     @pl.loop(0, ROWS // LANES)
     def _(b):
-        for d in (1, 2, 3):
-            o_copy(b, d, 0).wait_send()
+        o_spread(b).drain()
+
+    for flow in (scatter3, scatter2, scatter4, y_spread, x_spread):
+        flow.drain()
 
     y_store.wait()
     x_store.wait()

time: 284 us -> 236 us (0.83)
  Pallas kernels: 250 us -> 204 us
    pallas_call x1, Pallas kernels: 250 us -> 204 us  [run_block(): pl.pallas_call(kernel, out_shape=(jax.ShapeDtypeStruct((3, LANES, 256), F...]
where the time goes in v2:
time: 236 us
  Pallas kernels  204 us (86%)
  local copies, waits for them, and re-layouts  15 us (6%)
  other arithmetic  12.9 us (5%)
  between operations  3.63 us (2%)
    pallas_call x1, Pallas kernels, run_block(): pl.pallas_call(kernel, out_shape=(jax.ShapeDtypeStruct((3, LANES, 256), F...  204 us
    convert_element_type x8, other arithmetic, adam_step(): return [updated, mean_new, square_new, updated.astype(jnp.bfloat16)]  8.49 us
    unnamed x83, local copies, waits for them, and re-layouts  6.77 us

profile of v2, /device:TPU:0, one launch (start us, length us, event | category | flops | bytes accessed | tf_op | source)
XLA Modules:
  0.0 235.8 jit_solution(16767375057359669586)
XLA Ops:
  1.4 0.8 reshape.158
  2.1 0.8 copy.93
  3.0 1.3 concatenate.3.refs_2_
  4.3 1.4 multiply_bitcast_fusion
  5.7 1.2 pad.12.refs_1_
  6.9 0.5 copy-done.3
  7.5 1.2 pad.11.refs_0_
  8.9 204.3 %block_step.1 = (f32[3,128,256]{2,1,0:T(8,128)}, f32[256,128]{1,0:T(8,128)}, f32[128,1024]{1,0:T(8,128)}, f32[1024,128]{1,0:T(8,128)}, f32[8,1024]{1,0:T(8,128)}...) custom-call(bf16[640,1024]{1,0:T(8,128)(2,1)} %pad.11.refs_0_, ...), custom_call_target="tpu_custom_call" | custom-call | tf_op jit(solution)/shard_map/block_step/pallas_call | solution.py:1252
  213.2 1.2 slice.38
  215.1 0.7 slice_reduce_fusion.1
  216.0 0.7 constant_dynamic-slice_fusion.1
  216.6 0.8 slice_reduce_fusion
  217.7 0.6 fusion.32
  218.3 0.6 fusion.12
  219.0 0.7 fusion.28
  219.7 0.6 fusion.16
  220.3 1.7 fusion.26
  222.0 3.0 %bitcast_convert_fusion = (f32[1,577,1024]{2,1,0:T(8,128)S(1)}, bf16[1,577,1024]{2,1,0:T(8,128)(2,1)}) fusion(bf16[640,1024]{1,0:T(8,128)(2,1)} %get-tuple-element.60, bf16[640,1024]{1,0:T(8,128)(2,1)} %get-tuple-element.59), kind=kLoop, calls=%fused_computation | loop fusion | flops 590848 | bytes 5908480 | tf_op jit(solution)/shard_map/reshape | solution.py:1311
  225.1 3.8 %copy.95 = f32[1,577,1024]{2,0,1:T(1,128)} copy(f32[1,577,1024]{2,1,0:T(8,128)S(1)} %get-tuple-element.233) | data formatting | bytes 4726784
  229.0 1.3 fusion.30
  230.4 0.3 copy-done.5
  231.0 1.5 fusion.14
  232.5 0.5 copy-done.7
  233.1 1.5 fusion.18
  (83 shorter events, 1.1 us)
Async XLA Ops:
  8.6 209.0 %copy-start.29 = (f32[128]{0:T(128)S(1)}, f32[128]{0:T(128)}, u32[]{:S(2)}) copy-start(f32[128]{0:T(128)} %param.55) | copy-start | bytes 1540
  8.6 209.0 %copy-start.30 = (f32[128]{0:T(128)S(1)}, f32[128]{0:T(128)}, u32[]{:S(2)}) copy-start(f32[128]{0:T(128)} %param.66) | copy-start | bytes 1540
  8.6 209.0 %copy-start.31 = (f32[128]{0:T(128)S(1)}, f32[128]{0:T(128)}, u32[]{:S(2)}) copy-start(f32[128]{0:T(128)} %param.54) | copy-start | bytes 1540
  8.7 209.6 %copy-start.24 = (f32[128]{0:T(128)S(1)}, f32[128]{0:T(128)}, u32[]{:S(2)}) copy-start(f32[128]{0:T(128)} %param.47) | copy-start | bytes 1540
  8.7 209.6 %copy-start.25 = (f32[128]{0:T(128)S(1)}, f32[128]{0:T(128)}, u32[]{:S(2)}) copy-start(f32[128]{0:T(128)} %param.48) | copy-start | bytes 1540
  8.7 209.6 %copy-start.26 = (f32[128]{0:T(128)S(1)}, f32[128]{0:T(128)}, u32[]{:S(2)}) copy-start(f32[128]{0:T(128)} %param.49) | copy-start | bytes 1540
  8.7 209.6 %copy-start.27 = (f32[128]{0:T(128)S(1)}, f32[128]{0:T(128)}, u32[]{:S(2)}) copy-start(f32[128]{0:T(128)} %param.53) | copy-start | bytes 1540
  8.7 209.6 %copy-start.32 = (f32[128]{0:T(128)S(1)}, f32[128]{0:T(128)}, u32[]{:S(2)}) copy-start(f32[128]{0:T(128)} %param.77) | copy-start | bytes 1540
  8.7 209.6 %copy-start.33 = (f32[128]{0:T(128)S(1)}, f32[128]{0:T(128)}, u32[]{:S(2)}) copy-start(f32[128]{0:T(128)} %param.65) | copy-start | bytes 1540
  8.7 209.6 %copy-start.34 = (f32[128]{0:T(128)S(1)}, f32[128]{0:T(128)}, u32[]{:S(2)}) copy-start(f32[128]{0:T(128)} %param.73) | copy-start | bytes 1540
  8.7 209.6 %copy-start.35 = (f32[128]{0:T(128)S(1)}, f32[128]{0:T(128)}, u32[]{:S(2)}) copy-start(f32[128]{0:T(128)} %param.61) | copy-start | bytes 1540
  8.8 209.6 %copy-start.36 = (f32[128]{0:T(128)S(1)}, f32[128]{0:T(128)}, u32[]{:S(2)}) copy-start(f32[128]{0:T(128)} %param.72) | copy-start | bytes 1540
  8.8 209.5 %copy-start.37 = (f32[128]{0:T(128)S(1)}, f32[128]{0:T(128)}, u32[]{:S(2)}) copy-start(f32[128]{0:T(128)} %param.60) | copy-start | bytes 1540
  8.8 209.5 %copy-start.38 = (f32[128]{0:T(128)S(1)}, f32[128]{0:T(128)}, u32[]{:S(2)}) copy-start(f32[128]{0:T(128)} %param.71) | copy-start | bytes 1540
  8.8 209.5 %copy-start.39 = (f32[128]{0:T(128)S(1)}, f32[128]{0:T(128)}, u32[]{:S(2)}) copy-start(f32[128]{0:T(128)} %param.59) | copy-start | bytes 1540
  8.8 210.2 %copy-start.17 = (f32[2,4,8]{2,1,0:T(4,128)S(1)}, f32[2,4,8]{2,1,0:T(4,128)}, u32[]{:S(2)}) copy-start(f32[2,4,8]{2,1,0:T(4,128)} %param.45) | copy-start | bytes 772
  8.8 210.2 %copy-start.20 = (f32[2,4,8]{2,1,0:T(4,128)S(1)}, f32[2,4,8]{2,1,0:T(4,128)}, u32[]{:S(2)}) copy-start(f32[2,4,8]{2,1,0:T(4,128)} %param.69) | copy-start | bytes 772
  8.8 210.1 %copy-start.21 = (f32[2,4,8]{2,1,0:T(4,128)S(1)}, f32[2,4,8]{2,1,0:T(4,128)}, u32[]{:S(2)}) copy-start(f32[2,4,8]{2,1,0:T(4,128)} %param.57) | copy-start | bytes 772
  8.8 210.8 %copy-start.16 = (f32[16,8]{0,1:T(8,128)S(1)}, f32[16,8]{0,1:T(8,128)}, u32[]{:S(2)}) copy-start(f32[16,8]{0,1:T(8,128)} %param.51) | copy-start | bytes 1540
  8.9 210.8 %copy-start.18 = (f32[16,8]{0,1:T(8,128)S(1)}, f32[16,8]{0,1:T(8,128)}, u32[]{:S(2)}) copy-start(f32[16,8]{0,1:T(8,128)} %param.75) | copy-start | bytes 1540
  8.9 210.8 %copy-start.19 = (f32[16,8]{0,1:T(8,128)S(1)}, f32[16,8]{0,1:T(8,128)}, u32[]{:S(2)}) copy-start(f32[16,8]{0,1:T(8,128)} %param.63) | copy-start | bytes 1540
  8.9 211.4 %copy-start.10 = (f32[256,128]{1,0:T(8,128)S(1)}, f32[256,128]{1,0:T(8,128)}, u32[]{:S(2)}) copy-start(f32[256,128]{1,0:T(8,128)} %refs_4_.1) | copy-start | bytes 393220
  8.9 211.4 %copy-start.14 = (f32[256,128]{1,0:T(8,128)S(1)}, f32[256,128]{1,0:T(8,128)}, u32[]{:S(2)}) copy-start(f32[256,128]{1,0:T(8,128)} %param.70) | copy-start | bytes 393220
  8.9 211.4 %copy-start.15 = (f32[256,128]{1,0:T(8,128)S(1)}, f32[256,128]{1,0:T(8,128)}, u32[]{:S(2)}) copy-start(f32[256,128]{1,0:T(8,128)} %param.58) | copy-start | bytes 393220
  (16 other events, 658.0 us)
